TPU v7x, 32 devices: a whole 2x2x4 slice. The times are simulated.
32 devices in a mesh: seq: 8 (over z, x), ch: 4 (over y, core).
Axes of the slice: x: 2, y: 2, z: 4, core: 2. Of those that a mesh axis runs over, the one named last changes fastest.
Arguments:
- values: float32 [2048, 1024], P('seq', 'ch'), may hold values from -6 to 6
- gates: float32 [2048, 1024], P('seq', 'ch'), may hold values from -6 to 6
- filter_taps: float32 [4096, 1024], P('seq', 'ch'), may hold values from -0.09375 to 0.09375
- skip: float32 [1024], P('ch'), may hold values from 0.5 to 2
- out_weight: bfloat16 [1024, 2048], P(None, 'ch'), may hold values from -0.1875 to 0.1875
Outputs:
- mixed: float32 [2048, 2048], P('seq', 'ch')
All inputs are finite; a program needn't handle non-finite values.
Results may differ from a plain program's by a relative error of at most 0.0058.
Values may be sent and summed in bfloat16 or wider, within the bound.
A program may use at most 64 MiB of HBM per device.

v0:
```python
import functools
import math

import jax
import jax.numpy as jnp
from jax import lax
from jax.experimental import pallas as pl
from jax.experimental.pallas import tpu as pltpu
from jax.sharding import PartitionSpec as P

HIGHEST = lax.Precision.HIGHEST
MESH = pl.DeviceIdType.MESH
LANES = 128
TILE = 16
BUILD_UNROLL = 8
CONV_UNROLL = 16


def split_length(length):
    leading = 1
    for factor in range(1, math.isqrt(length) + 1):
        if length % factor == 0:
            leading = factor
    return (leading, length // leading)


def phase_table(count_rows, count_cols, modulus):
    row_ids = jnp.arange(count_rows, dtype=jnp.int32)
    col_ids = jnp.arange(count_cols, dtype=jnp.int32)
    wrapped = row_ids[:, None] * col_ids[None, :] % modulus
    phases = 2.0 * math.pi / modulus * wrapped.astype(jnp.float32)
    return (jnp.cos(phases), jnp.sin(phases))


def complex_form(cosine, sine):
    upper = jnp.stack([cosine, -sine], axis=1)
    lower = jnp.stack([sine, cosine], axis=1)
    return jnp.stack([upper, lower], axis=0)


def transform_tables(length):
    rows_lead, rows_tail = split_length(length)
    cos_lead, sin_lead = phase_table(rows_lead, rows_lead, rows_lead)
    cos_tail, sin_tail = phase_table(rows_tail, rows_tail, rows_tail)
    cos_twist, sin_twist = phase_table(rows_lead, rows_tail, length)
    lead_table = jnp.stack([cos_lead, -sin_lead])
    tail_forward = complex_form(cos_tail, -sin_tail)
    tail_inverse = complex_form(cos_tail, sin_tail)
    return (
        lead_table,
        tail_forward,
        tail_inverse,
        cos_twist,
        sin_twist,
        rows_lead,
        rows_tail,
        length,
    )


def twist_rows(section, cosine, sine):
    real_part = section[0] * cosine[None] - section[1] * sine[None]
    imag_part = section[0] * sine[None] + section[1] * cosine[None]
    return jnp.stack([real_part, imag_part])


def forward_rows(rows, tables):
    lead_table, tail_forward, tail_inverse, cos_twist, sin_twist, rows_lead, rows_tail, length = (
        tables
    )
    signal = jnp.concatenate([rows, jnp.zeros_like(rows)], axis=1).reshape(
        rows.shape[0], rows_lead, rows_tail
    )
    section = jnp.einsum("pft,cts->pcfs", lead_table, signal, precision=HIGHEST)
    twisted = twist_rows(section, cos_twist, -sin_twist)
    return jnp.einsum("pgrs,rcfs->pcfg", tail_forward, twisted, precision=HIGHEST)


def inverse_rows(spectrum, tables):
    lead_table, tail_forward, tail_inverse, cos_twist, sin_twist, rows_lead, rows_tail, length = (
        tables
    )
    section = jnp.einsum("pgrs,rcfs->pcfg", tail_inverse, spectrum, precision=HIGHEST)
    twisted = twist_rows(section, cos_twist, sin_twist)
    signal = jnp.einsum("rft,rcfs->cts", lead_table, twisted, precision=HIGHEST) / length
    return signal.reshape(signal.shape[0], length)


def product(left, right):
    real_part = left[0] * right[0] - left[1] * right[1]
    imag_part = left[0] * right[1] + left[1] * right[0]
    return jnp.stack([real_part, imag_part])


def body(values, gates, filter_taps, skip, out_weight):
    block_rows, width = values.shape
    whole_filter = lax.all_gather(filter_taps, "seq", axis=0, tiled=True)
    devices = lax.axis_size("seq")
    narrow = width // devices
    whole_rows = lax.all_to_all(values.T, "seq", split_axis=0, concat_axis=1, tiled=True)
    total_rows = whole_rows.shape[1]
    own_taps = lax.dynamic_slice_in_dim(whole_filter, lax.axis_index("seq") * narrow, narrow, 1).T
    used_taps = min(own_taps.shape[1], total_rows)
    own_taps = own_taps[:, :used_taps]
    taps_rows = jnp.concatenate(
        [own_taps, jnp.zeros((narrow, total_rows - used_taps), jnp.float32)], axis=1
    )
    row_tables = transform_tables(2 * total_rows)
    spectrum = product(forward_rows(whole_rows, row_tables), forward_rows(taps_rows, row_tables))
    convolved_rows = inverse_rows(spectrum, row_tables)[:, :total_rows]
    convolved = lax.all_to_all(convolved_rows, "seq", split_axis=1, concat_axis=0, tiled=True).T
    hidden = (gates * (convolved + skip[None, :] * values)).astype(jnp.bfloat16)
    return jnp.dot(
        lax.all_gather(hidden, "ch", axis=1, tiled=True),
        out_weight,
        preferred_element_type=jnp.float32,
    )


def toeplitz_kernel(
    tap_sources,
    values_hbm,
    gates_hbm,
    taps_hbm,
    skip_ref,
    weight_hbm,
    out_hbm,
    values_ref,
    gates_ref,
    taps_ref,
    out_ref,
    x_out,
    h_out,
    x_in,
    h_in,
    x_rows,
    toeplitz,
    h_blocks,
    y_blocks,
    y_out,
    y_in,
    hidden,
    weight,
    load_sem,
    out_sem,
    x_send,
    x_recv,
    h_send,
    h_recv,
    y_send,
    y_recv,
    g_send,
    g_recv,
):
    seq_size, narrow, block_rows = x_out.shape
    tap_rows = h_out.shape[2]
    ch_size, _, width = hidden.shape
    blocks = x_rows.shape[0] // narrow
    per = block_rows // LANES
    me, lane_group = lax.axis_index("seq"), lax.axis_index("ch")
    f32, bf16 = jnp.float32, jnp.bfloat16

    loads = [
        pltpu.make_async_copy(source, target, load_sem.at[place])
        for place, (source, target) in enumerate(
            (
                (values_hbm, values_ref),
                (taps_hbm, taps_ref),
                (gates_hbm, gates_ref),
                (weight_hbm, weight),
            )
        )
    ]
    for load in loads:
        load.start()

    barrier = pltpu.get_barrier_semaphore()
    for step in range(1, seq_size):
        pl.semaphore_signal(
            barrier, inc=1, device_id={"seq": lax.rem(me + step, seq_size)}, device_id_type=MESH
        )
    for step in range(1, ch_size):
        pl.semaphore_signal(
            barrier, inc=1, device_id={"ch": lax.rem(lane_group + step, ch_size)}, device_id_type=MESH
        )

    h_blocks[...] = jnp.zeros_like(h_blocks)
    loads[0].wait()
    x_out[...] = values_ref[...].T.astype(bf16).reshape(x_out.shape)
    pl.semaphore_wait(barrier, seq_size + ch_size - 2)

    groups = narrow // TILE
    x_copies = []
    for group in range(groups):
        part = pl.ds(group * TILE, TILE)
        for step in range(1, seq_size):
            to = lax.rem(me + step, seq_size)
            copy = pltpu.make_async_remote_copy(
                x_out.at[to, part], x_in.at[me, part],
                x_send.at[group, step], x_recv.at[group, step],
                device_id={"seq": to}, device_id_type=MESH,
            )
            copy.start()
            x_copies.append(copy)

    loads[1].wait()

    def tap_copy(group, step):
        to = lax.rem(me + step, seq_size)
        part = pl.ds(group * TILE, TILE)
        return pltpu.make_async_remote_copy(
            h_out.at[to, part], h_in.at[me, part], h_send.at[group, step], h_recv.at[group, me],
            device_id={"seq": to}, device_id_type=MESH,
        )

    @pl.when(me < tap_sources)
    def _():
        h_out[...] = taps_ref[...].T.astype(bf16).reshape(h_out.shape)
        for group in range(groups):
            for step in range(1, seq_size):
                tap_copy(group, step).start()
        h_in[me] = h_out[me]

    x_in[me] = x_out[me]
    row_ids = lax.broadcasted_iota(jnp.int32, (LANES, LANES), 0)
    col_ids = lax.broadcasted_iota(jnp.int32, (LANES, LANES), 1)

    def build_one(channel):
        before = jnp.zeros((LANES, LANES), f32)
        rows = x_rows[pl.ds(pl.multiple_of(channel * blocks, blocks), blocks), :]
        for block in range(blocks):
            row = rows[block : block + 1]
            turned = pltpu.roll(
                jnp.broadcast_to(row, (LANES, LANES)), 0, 1, stride=1, stride_axis=0
            )
            toeplitz[channel, block * LANES : (block + 1) * LANES, :] = jnp.where(
                col_ids >= row_ids, turned, before
            ).astype(bf16)
            before = turned

    def build(turn, carry):
        for part in range(BUILD_UNROLL):
            build_one(turn * BUILD_UNROLL + part)
        return carry

    turns = TILE // BUILD_UNROLL
    for group in range(groups):
        for copy in x_copies[group * (seq_size - 1) : (group + 1) * (seq_size - 1)]:
            copy.wait_recv()
        for source in range(seq_size):
            for piece in range(per):
                x_rows[pl.ds(group * TILE * blocks + source * per + piece, TILE, stride=blocks), :] = x_in[
                    source, group * TILE : (group + 1) * TILE, piece * LANES : (piece + 1) * LANES
                ].astype(f32)
        lax.fori_loop(group * turns, (group + 1) * turns, build, 0)

    pieces = tap_rows // LANES
    flat_blocks = h_blocks.reshape(narrow * 2 * blocks, LANES)

    def take_taps(group):
        part = slice(group * TILE, (group + 1) * TILE)
        for source in range(tap_sources):
            @pl.when(me != source)
            def _():
                pltpu.make_async_remote_copy(
                    h_out.at[0, part], h_in.at[source, part], h_send.at[group, 0],
                    h_recv.at[group, source], device_id={"seq": source}, device_id_type=MESH,
                ).wait_recv()
        for source in range(tap_sources):
            for piece in range(pieces):
                first = group * TILE * 2 * blocks + blocks + source * pieces + piece
                flat_blocks[pl.ds(first, TILE, stride=2 * blocks), :] = h_in[
                    source, part, piece * LANES : (piece + 1) * LANES
                ].astype(f32)

    def convolve_one(channel):
        left = jnp.concatenate(
            [h_blocks[channel, blocks - lag : 2 * blocks - lag, :] for lag in range(blocks)], axis=1
        ).astype(bf16)
        y_blocks[pl.ds(pl.multiple_of(channel * blocks, blocks), blocks), :] = jnp.dot(
            left, toeplitz[channel], preferred_element_type=f32
        )

    def convolve(turn, carry):
        for part in range(CONV_UNROLL):
            convolve_one(turn * CONV_UNROLL + part)
        return carry

    turns = TILE // CONV_UNROLL
    for group in range(groups):
        take_taps(group)
        lax.fori_loop(group * turns, (group + 1) * turns, convolve, 0)
    for block in range(blocks):
        y_out[block // per, :, (block % per) * LANES : (block % per + 1) * LANES] = y_blocks[
            pl.ds(block, narrow, stride=blocks), :
        ].astype(bf16)
    y_copies = {}
    for piece in range(per):
        span = pl.ds(piece * LANES, LANES)
        for step in range(1, seq_size):
            to = lax.rem(me + step, seq_size)
            y_copies[piece, step] = pltpu.make_async_remote_copy(
                y_out.at[to, :, span], y_in.at[me, :, span],
                y_send.at[piece, step], y_recv.at[piece, step],
                device_id={"seq": to}, device_id_type=MESH,
            )
            y_copies[piece, step].start()
    y_in[me] = y_out[me]

    partner = lane_group + 1 - 2 * lax.rem(lane_group, 2)
    pairs = ch_size // 2

    def spread(kind, piece, slot, to):
        block = hidden.at[slot, pl.ds(piece * LANES, LANES)]
        copy = pltpu.make_async_remote_copy(
            block, block, g_send.at[kind, piece], g_recv.at[kind, piece],
            device_id={"ch": to}, device_id_type=MESH,
        )
        copy.start()
        g_copies.append(copy)
        return copy

    def add_product(piece, slot, first=False):
        rows = slice(piece * LANES, (piece + 1) * LANES)
        term = jnp.dot(hidden[slot, rows], weight[slot], preferred_element_type=f32)
        out_ref[rows] = term if first else out_ref[rows] + term

    g_copies, direct, relayed = [], {}, {}
    loads[2].wait()
    for piece in range(per):
        rows = slice(piece * LANES, (piece + 1) * LANES)
        for step in range(1, seq_size):
            y_copies[piece, step].wait_recv()
        convolved = y_in[:, :, rows].astype(f32).reshape(width, LANES).T
        hidden[lane_group, rows] = (
            gates_ref[rows] * (convolved + skip_ref[...] * values_ref[rows])
        ).astype(bf16)
        for pair in range(1, pairs):
            direct[pair, piece] = spread(
                2 * pair - 1, piece, lane_group, lax.rem(lane_group + 2 * pair, ch_size)
            )
        direct[0, piece] = spread(0, piece, lane_group, partner)
    loads[3].wait()
    for piece in range(per):
        add_product(piece, lane_group, True)
    for piece in range(per):
        direct[0, piece].wait_recv()
        add_product(piece, partner)
    for piece in range(per):
        for pair in range(1, pairs):
            slot = lax.rem(lane_group + ch_size - 2 * pair, ch_size)
            direct[pair, piece].wait_recv()
            relayed[pair, piece] = spread(2 * pair, piece, slot, partner)
            add_product(piece, slot)
    stores = []
    for piece in range(per):
        rows = pl.ds(piece * LANES, LANES)
        for pair in range(1, pairs):
            slot = lax.rem(partner + ch_size - 2 * pair, ch_size)
            relayed[pair, piece].wait_recv()
            add_product(piece, slot)
        store = pltpu.make_async_copy(out_ref.at[rows], out_hbm.at[rows], out_sem.at[piece])
        store.start()
        stores.append(store)
    for store in stores:
        store.wait()

    for copy in x_copies + list(y_copies.values()) + g_copies:
        copy.wait_send()

    @pl.when(me < tap_sources)
    def _():
        for group in range(groups):
            for step in range(1, seq_size):
                tap_copy(group, step).wait_send()


def toeplitz_body(values, gates, filter_taps, skip, out_weight):
    seq_size, ch_size = lax.axis_size("seq"), lax.axis_size("ch")
    block_rows, width = values.shape
    tap_rows = filter_taps.shape[0]
    narrow = width // seq_size
    total = block_rows * seq_size
    sources = min(tap_rows * seq_size, total) // tap_rows
    columns = out_weight.shape[1]
    f32, bf16 = jnp.float32, jnp.bfloat16
    vmem = pl.BlockSpec(memory_space=pltpu.VMEM)
    hbm = pl.BlockSpec(memory_space=pl.ANY)
    per = block_rows // LANES
    dma = pltpu.SemaphoreType.DMA
    return pl.pallas_call(
        functools.partial(toeplitz_kernel, sources),
        out_shape=jax.ShapeDtypeStruct((block_rows, columns), f32),
        in_specs=[hbm] * 3 + [vmem, hbm],
        out_specs=hbm,
        scratch_shapes=[
            pltpu.VMEM((block_rows, width), f32),
            pltpu.VMEM((block_rows, width), f32),
            pltpu.VMEM((tap_rows, width), f32),
            pltpu.VMEM((block_rows, columns), f32),
            pltpu.VMEM((seq_size, narrow, block_rows), bf16),
            pltpu.VMEM((seq_size, narrow, tap_rows), bf16),
            pltpu.VMEM((seq_size, narrow, block_rows), bf16),
            pltpu.VMEM((sources, narrow, tap_rows), bf16),
            pltpu.VMEM((narrow * (total // LANES), LANES), f32),
            pltpu.VMEM((narrow, total, LANES), bf16),
            pltpu.VMEM((narrow, 2 * (total // LANES), LANES), f32),
            pltpu.VMEM((narrow * (total // LANES), LANES), f32),
            pltpu.VMEM((seq_size, narrow, block_rows), bf16),
            pltpu.VMEM((seq_size, narrow, block_rows), bf16),
            pltpu.VMEM((ch_size, block_rows, width), bf16),
            pltpu.VMEM((ch_size, width, columns), bf16),
            dma((4,)),
            dma((per,)),
            dma((narrow // TILE, seq_size)),
            dma((narrow // TILE, seq_size)),
            dma((narrow // TILE, seq_size)),
            dma((narrow // TILE, sources)),
            dma((per, seq_size)),
            dma((per, seq_size)),
            dma((ch_size, per)),
            dma((ch_size, per)),
        ],
        compiler_params=pltpu.CompilerParams(
            collective_id=0, has_side_effects=True, vmem_limit_bytes=63000 * 1024
        ),
    )(
        values,
        gates,
        filter_taps,
        skip.reshape(1, width),
        out_weight.reshape(ch_size, width, columns),
    )


def local_body(values, gates, filter_taps, skip, out_weight):
    seq_size = lax.axis_size("seq")
    block_rows, width = values.shape
    tap_rows = filter_taps.shape[0]
    narrow = width // seq_size
    total = block_rows * seq_size
    fits = (
        width % (seq_size * TILE) == 0
        and lax.axis_size("ch") % 2 == 0
        and width % LANES == 0
        and block_rows % LANES == 0
        and total // LANES % 8 == 0
        and tap_rows % LANES == 0
        and total % tap_rows == 0
        and narrow * total * LANES * 2 <= 32 * 1024 * 1024
    )
    chosen = toeplitz_body if fits else body
    return chosen(values, gates, filter_taps, skip, out_weight)


def solution(mesh):
    placed = (P("seq", "ch"), P("seq", "ch"), P("seq", "ch"), P("ch"), P(None, "ch"))
    return jax.shard_map(
        local_body, mesh=mesh, in_specs=placed, out_specs=P("seq", "ch"), check_vma=False
    )
```

profile of v0, /device:TPU:1, one launch (start us, length us, event | category | flops | bytes accessed | tf_op | source)
XLA Modules:
  0.0 32.2 jit_solution(485170445405961947)
XLA Ops:
  0.0 30.3 %shard_map.55 = f32[256,512]{1,0:T(8,128)} custom-call(f32[256,256]{1,0:T(8,128)} %values_hbm.1, f32[256,256]{1,0:T(8,128)} %gates_hbm.1, f32[512,256]{1,0:T(8,128)} %taps_hbm.1, f32[1,256]{1,0:T(1,128)} %bitcast.3, bf16[4,256,512]{2,1,0:T(8,128)(2,1)} %bitcast.2), custom_call_target="tpu_custom_call" | custom-call | tf_op jit(solution)/shard_map/pallas_call | solution.py:391
  30.3 1.9 %copy.7 = f32[256,512]{1,0:T(8,128)} copy(f32[256,512]{1,0:T(8,128)} %shard_map.55) | data formatting | bytes 1048576
where the time goes:
time: 32.4 us; the launch traced here: 32.2 us
  Pallas kernels  30.3 us (94%)
  local copies, waits for them, and re-layouts  1.87 us (6%)
    pallas_call x1, Pallas kernels, toeplitz_body(): pl.pallas_call(functools.partial(toeplitz_kernel, sources), out_shape=jax...  30.3 us
    unnamed x1, local copies, waits for them, and re-layouts  1.87 us

commit v1 on v0

--- a/solution.py
+++ b/solution.py
@@ -3,6 +3,7 @@
 
 import jax
 import jax.numpy as jnp
+import numpy as np
 from jax import lax
 from jax.experimental import pallas as pl
 from jax.experimental.pallas import tpu as pltpu
@@ -12,8 +13,7 @@
 MESH = pl.DeviceIdType.MESH
 LANES = 128
 TILE = 16
-BUILD_UNROLL = 8
-CONV_UNROLL = 16
+PAIR = 2
 
 
 def split_length(length):
@@ -117,13 +117,31 @@
     )
 
 
-def toeplitz_kernel(
+def block_tables():
+    size = 2 * LANES
+    place = np.arange(size)[:, None]
+    odd = 2 * np.arange(LANES)[None, :] + 1
+    angle = np.pi / size * (place * odd % (2 * size))
+    forward = np.concatenate([np.cos(angle), -np.sin(angle)], axis=1)
+    inverse = forward[LANES:].T / LANES
+
+    def two_parts(table, axis):
+        high = table.astype(jnp.bfloat16)
+        low = (table - high.astype(np.float64)).astype(jnp.bfloat16)
+        return np.concatenate([high, low], axis=axis)
+
+    return two_parts(forward, 0), two_parts(inverse, 1)
+
+
+def block_kernel(
     tap_sources,
     values_hbm,
     gates_hbm,
     taps_hbm,
     skip_ref,
     weight_hbm,
+    forward_hbm,
+    inverse_hbm,
     out_hbm,
     values_ref,
     gates_ref,
@@ -133,14 +151,15 @@
     h_out,
     x_in,
     h_in,
-    x_rows,
-    toeplitz,
-    h_blocks,
-    y_blocks,
+    x_waves,
+    h_waves,
+    y_waves,
     y_out,
     y_in,
     hidden,
     weight,
+    forward,
+    inverse,
     load_sem,
     out_sem,
     x_send,
@@ -155,7 +174,6 @@
     seq_size, narrow, block_rows = x_out.shape
     tap_rows = h_out.shape[2]
     ch_size, _, width = hidden.shape
-    blocks = x_rows.shape[0] // narrow
     per = block_rows // LANES
     me, lane_group = lax.axis_index("seq"), lax.axis_index("ch")
     f32, bf16 = jnp.float32, jnp.bfloat16
@@ -166,6 +184,8 @@
             (
                 (values_hbm, values_ref),
                 (taps_hbm, taps_ref),
+                (forward_hbm, forward),
+                (inverse_hbm, inverse),
                 (gates_hbm, gates_ref),
                 (weight_hbm, weight),
             )
@@ -184,127 +204,161 @@
             barrier, inc=1, device_id={"ch": lax.rem(lane_group + step, ch_size)}, device_id_type=MESH
         )
 
-    h_blocks[...] = jnp.zeros_like(h_blocks)
     loads[0].wait()
     x_out[...] = values_ref[...].T.astype(bf16).reshape(x_out.shape)
-    pl.semaphore_wait(barrier, seq_size + ch_size - 2)
-
-    groups = narrow // TILE
-    x_copies = []
-    for group in range(groups):
-        part = pl.ds(group * TILE, TILE)
-        for step in range(1, seq_size):
-            to = lax.rem(me + step, seq_size)
-            copy = pltpu.make_async_remote_copy(
-                x_out.at[to, part], x_in.at[me, part],
-                x_send.at[group, step], x_recv.at[group, step],
-                device_id={"seq": to}, device_id_type=MESH,
-            )
-            copy.start()
-            x_copies.append(copy)
-
+    x_in[me] = x_out[me]
     loads[1].wait()
-
-    def tap_copy(group, step):
-        to = lax.rem(me + step, seq_size)
-        part = pl.ds(group * TILE, TILE)
-        return pltpu.make_async_remote_copy(
-            h_out.at[to, part], h_in.at[me, part], h_send.at[group, step], h_recv.at[group, me],
-            device_id={"seq": to}, device_id_type=MESH,
-        )
 
     @pl.when(me < tap_sources)
     def _():
         h_out[...] = taps_ref[...].T.astype(bf16).reshape(h_out.shape)
-        for group in range(groups):
-            for step in range(1, seq_size):
-                tap_copy(group, step).start()
         h_in[me] = h_out[me]
 
-    x_in[me] = x_out[me]
-    row_ids = lax.broadcasted_iota(jnp.int32, (LANES, LANES), 0)
-    col_ids = lax.broadcasted_iota(jnp.int32, (LANES, LANES), 1)
-
-    def build_one(channel):
-        before = jnp.zeros((LANES, LANES), f32)
-        rows = x_rows[pl.ds(pl.multiple_of(channel * blocks, blocks), blocks), :]
-        for block in range(blocks):
-            row = rows[block : block + 1]
-            turned = pltpu.roll(
-                jnp.broadcast_to(row, (LANES, LANES)), 0, 1, stride=1, stride_axis=0
-            )
-            toeplitz[channel, block * LANES : (block + 1) * LANES, :] = jnp.where(
-                col_ids >= row_ids, turned, before
-            ).astype(bf16)
-            before = turned
-
-    def build(turn, carry):
-        for part in range(BUILD_UNROLL):
-            build_one(turn * BUILD_UNROLL + part)
-        return carry
-
-    turns = TILE // BUILD_UNROLL
-    for group in range(groups):
-        for copy in x_copies[group * (seq_size - 1) : (group + 1) * (seq_size - 1)]:
-            copy.wait_recv()
-        for source in range(seq_size):
-            for piece in range(per):
-                x_rows[pl.ds(group * TILE * blocks + source * per + piece, TILE, stride=blocks), :] = x_in[
-                    source, group * TILE : (group + 1) * TILE, piece * LANES : (piece + 1) * LANES
-                ].astype(f32)
-        lax.fori_loop(group * turns, (group + 1) * turns, build, 0)
-
-    pieces = tap_rows // LANES
-    flat_blocks = h_blocks.reshape(narrow * 2 * blocks, LANES)
-
-    def take_taps(group):
-        part = slice(group * TILE, (group + 1) * TILE)
-        for source in range(tap_sources):
+    rounds = seq_size // PAIR
+    home, side = me // PAIR, lax.rem(me, PAIR)
+    targets = []
+    for near in [rounds // 2] + [n for k in range(1, (rounds + 1) // 2) for n in (rounds - k, k)] + [0]:
+        for turn in range(PAIR):
+            if near or turn:
+                targets.append(
+                    lax.rem(home + near, rounds) * PAIR + lax.rem(side + turn, PAIR)
+                )
+
+    def x_copy(place, to):
+        return pltpu.make_async_remote_copy(
+            x_out.at[to], x_in.at[me], x_send.at[place], x_recv.at[me],
+            device_id={"seq": to}, device_id_type=MESH,
+        )
+
+    def h_copy(place, to):
+        return pltpu.make_async_remote_copy(
+            h_out.at[to], h_in.at[me], h_send.at[place], h_recv.at[me],
+            device_id={"seq": to}, device_id_type=MESH,
+        )
+
+    pl.semaphore_wait(barrier, seq_size + ch_size - 2)
+    x_copies = [x_copy(place, to) for place, to in enumerate(targets)]
+    for copy in x_copies:
+        copy.start()
+
+    @pl.when(me < tap_sources)
+    def _():
+        for place, to in enumerate(targets):
+            h_copy(place, to).start()
+
+    for load in loads[2:4]:
+        load.wait()
+
+    def take_taps(source):
+        @pl.when(me != source)
+        def _():
+            pltpu.make_async_remote_copy(
+                h_out.at[0], h_in.at[source], h_send.at[0], h_recv.at[source],
+                device_id={"seq": source}, device_id_type=MESH,
+            ).wait_recv()
+        pieces = tap_rows // LANES
+        rows = jnp.concatenate(
+            [h_in[source, :, piece * LANES : (piece + 1) * LANES] for piece in range(pieces)], axis=0
+        )
+        table = jnp.concatenate(
+            [forward[:LANES], forward[2 * LANES : 3 * LANES]], axis=0
+        )
+        waves = jnp.dot(
+            jnp.concatenate([rows, rows], axis=1), table, preferred_element_type=f32
+        )
+        h_waves[source * pieces : (source + 1) * pieces] = waves.reshape(
+            pieces, narrow, 2 * LANES
+        )
+
+    def take_values(first):
+        for source in range(first, first + PAIR):
             @pl.when(me != source)
             def _():
                 pltpu.make_async_remote_copy(
-                    h_out.at[0, part], h_in.at[source, part], h_send.at[group, 0],
-                    h_recv.at[group, source], device_id={"seq": source}, device_id_type=MESH,
+                    x_out.at[0], x_in.at[source], x_send.at[0], x_recv.at[source],
+                    device_id={"seq": source}, device_id_type=MESH,
                 ).wait_recv()
-        for source in range(tap_sources):
-            for piece in range(pieces):
-                first = group * TILE * 2 * blocks + blocks + source * pieces + piece
-                flat_blocks[pl.ds(first, TILE, stride=2 * blocks), :] = h_in[
-                    source, part, piece * LANES : (piece + 1) * LANES
-                ].astype(f32)
-
-    def convolve_one(channel):
-        left = jnp.concatenate(
-            [h_blocks[channel, blocks - lag : 2 * blocks - lag, :] for lag in range(blocks)], axis=1
-        ).astype(bf16)
-        y_blocks[pl.ds(pl.multiple_of(channel * blocks, blocks), blocks), :] = jnp.dot(
-            left, toeplitz[channel], preferred_element_type=f32
-        )
-
-    def convolve(turn, carry):
-        for part in range(CONV_UNROLL):
-            convolve_one(turn * CONV_UNROLL + part)
-        return carry
-
-    turns = TILE // CONV_UNROLL
-    for group in range(groups):
-        take_taps(group)
-        lax.fori_loop(group * turns, (group + 1) * turns, convolve, 0)
-    for block in range(blocks):
-        y_out[block // per, :, (block % per) * LANES : (block % per + 1) * LANES] = y_blocks[
-            pl.ds(block, narrow, stride=blocks), :
-        ].astype(bf16)
-    y_copies = {}
-    for piece in range(per):
+        if first:
+            before = x_in[first - 1, :, block_rows - LANES :]
+        else:
+            before = jnp.zeros((narrow, LANES), bf16)
+        rows = []
+        for source in range(first, first + PAIR):
+            for piece in range(per):
+                here = x_in[source, :, piece * LANES : (piece + 1) * LANES]
+                rows.append(jnp.concatenate([before, here, before, here], axis=1))
+                before = here
+        waves = jnp.dot(
+            jnp.concatenate(rows, axis=0), forward[...], preferred_element_type=f32
+        )
+        x_waves[first * per : (first + PAIR) * per] = waves.reshape(
+            PAIR * per, narrow, 2 * LANES
+        )
+
+    def multiply(first):
+        start = first * per
+        count = PAIR * per
+        for part in range(narrow // TILE):
+            rows = slice(part * TILE, (part + 1) * TILE)
+            cache = {}
+
+            def x_part(block):
+                if block not in cache:
+                    cache[block] = (x_waves[block, rows, :LANES], x_waves[block, rows, LANES:])
+                return cache[block]
+
+            sums = [None] * count
+            for lag in range(start + count):
+                h_real, h_imag = h_waves[lag, rows, :LANES], h_waves[lag, rows, LANES:]
+                for spot in range(count):
+                    block = start + spot - lag
+                    if block < 0:
+                        continue
+                    x_real, x_imag = x_part(block)
+                    real = x_real * h_real - x_imag * h_imag
+                    imag = x_real * h_imag + x_imag * h_real
+                    if sums[spot] is None:
+                        sums[spot] = (real, imag)
+                    else:
+                        sums[spot] = (sums[spot][0] + real, sums[spot][1] + imag)
+            for spot in range(count):
+                y_waves[spot, rows, :LANES] = sums[spot][0]
+                y_waves[spot, rows, LANES:] = sums[spot][1]
+
+    def y_copy(target, piece):
         span = pl.ds(piece * LANES, LANES)
-        for step in range(1, seq_size):
-            to = lax.rem(me + step, seq_size)
-            y_copies[piece, step] = pltpu.make_async_remote_copy(
-                y_out.at[to, :, span], y_in.at[me, :, span],
-                y_send.at[piece, step], y_recv.at[piece, step],
-                device_id={"seq": to}, device_id_type=MESH,
-            )
-            y_copies[piece, step].start()
+        return pltpu.make_async_remote_copy(
+            y_out.at[target, :, span], y_in.at[me, :, span],
+            y_send.at[target, piece], y_recv.at[me, piece],
+            device_id={"seq": target}, device_id_type=MESH,
+        )
+
+    def give_back(first):
+        waves = y_waves[...].reshape(PAIR * per * narrow, 2 * LANES)
+        high = waves.astype(bf16)
+        low = (waves - high.astype(f32)).astype(bf16)
+        both = jnp.dot(high, inverse[...], preferred_element_type=f32)
+        rest = jnp.dot(low, inverse[:, :LANES], preferred_element_type=f32)
+        convolved = (both[:, :LANES] + both[:, LANES:] + rest).astype(bf16)
+        for spot in range(PAIR * per):
+            source, piece = first + spot // per, spot % per
+            y_out[source, :, piece * LANES : (piece + 1) * LANES] = convolved[
+                spot * narrow : (spot + 1) * narrow
+            ]
+        for piece in range(per):
+            for target in range(first, first + PAIR):
+                @pl.when(me != target)
+                def _():
+                    y_copy(target, piece).start()
+
+    taken = 0
+    for first in range(0, seq_size, PAIR):
+        while taken < tap_sources and taken * tap_rows < (first + PAIR) * block_rows:
+            take_taps(taken)
+            taken += 1
+        take_values(first)
+        multiply(first)
+        give_back(first)
     y_in[me] = y_out[me]
 
     partner = lane_group + 1 - 2 * lax.rem(lane_group, 2)
@@ -326,11 +380,18 @@
         out_ref[rows] = term if first else out_ref[rows] + term
 
     g_copies, direct, relayed = [], {}, {}
-    loads[2].wait()
+    loads[4].wait()
     for piece in range(per):
         rows = slice(piece * LANES, (piece + 1) * LANES)
-        for step in range(1, seq_size):
-            y_copies[piece, step].wait_recv()
+        for source in range(seq_size):
+            @pl.when(me != source)
+            def _():
+                span = pl.ds(piece * LANES, LANES)
+                pltpu.make_async_remote_copy(
+                    y_out.at[source, :, span], y_in.at[source, :, span],
+                    y_send.at[source, piece], y_recv.at[source, piece],
+                    device_id={"seq": source}, device_id_type=MESH,
+                ).wait_recv()
         convolved = y_in[:, :, rows].astype(f32).reshape(width, LANES).T
         hidden[lane_group, rows] = (
             gates_ref[rows] * (convolved + skip_ref[...] * values_ref[rows])
@@ -340,7 +401,7 @@
                 2 * pair - 1, piece, lane_group, lax.rem(lane_group + 2 * pair, ch_size)
             )
         direct[0, piece] = spread(0, piece, lane_group, partner)
-    loads[3].wait()
+    loads[5].wait()
     for piece in range(per):
         add_product(piece, lane_group, True)
     for piece in range(per):
@@ -365,17 +426,21 @@
     for store in stores:
         store.wait()
 
-    for copy in x_copies + list(y_copies.values()) + g_copies:
+    for copy in x_copies + g_copies:
         copy.wait_send()
+    for target in range(seq_size):
+        @pl.when(me != target)
+        def _():
+            for piece in range(per):
+                y_copy(target, piece).wait_send()
 
     @pl.when(me < tap_sources)
     def _():
-        for group in range(groups):
-            for step in range(1, seq_size):
-                tap_copy(group, step).wait_send()
-
-
-def toeplitz_body(values, gates, filter_taps, skip, out_weight):
+        for place, to in enumerate(targets):
+            h_copy(place, to).wait_send()
+
+
+def block_body(values, gates, filter_taps, skip, out_weight):
     seq_size, ch_size = lax.axis_size("seq"), lax.axis_size("ch")
     block_rows, width = values.shape
     tap_rows = filter_taps.shape[0]
@@ -388,10 +453,11 @@
     hbm = pl.BlockSpec(memory_space=pl.ANY)
     per = block_rows // LANES
     dma = pltpu.SemaphoreType.DMA
+    forward, inverse = block_tables()
     return pl.pallas_call(
-        functools.partial(toeplitz_kernel, sources),
+        functools.partial(block_kernel, sources),
         out_shape=jax.ShapeDtypeStruct((block_rows, columns), f32),
-        in_specs=[hbm] * 3 + [vmem, hbm],
+        in_specs=[hbm] * 3 + [vmem] + [hbm] * 3,
         out_specs=hbm,
         scratch_shapes=[
             pltpu.VMEM((block_rows, width), f32),
@@ -402,22 +468,23 @@
             pltpu.VMEM((seq_size, narrow, tap_rows), bf16),
             pltpu.VMEM((seq_size, narrow, block_rows), bf16),
             pltpu.VMEM((sources, narrow, tap_rows), bf16),
-            pltpu.VMEM((narrow * (total // LANES), LANES), f32),
-            pltpu.VMEM((narrow, total, LANES), bf16),
-            pltpu.VMEM((narrow, 2 * (total // LANES), LANES), f32),
-            pltpu.VMEM((narrow * (total // LANES), LANES), f32),
+            pltpu.VMEM((total // LANES, narrow, 2 * LANES), f32),
+            pltpu.VMEM((total // LANES, narrow, 2 * LANES), f32),
+            pltpu.VMEM((PAIR * per, narrow, 2 * LANES), f32),
             pltpu.VMEM((seq_size, narrow, block_rows), bf16),
             pltpu.VMEM((seq_size, narrow, block_rows), bf16),
             pltpu.VMEM((ch_size, block_rows, width), bf16),
             pltpu.VMEM((ch_size, width, columns), bf16),
-            dma((4,)),
+            pltpu.VMEM(forward.shape, bf16),
+            pltpu.VMEM(inverse.shape, bf16),
+            dma((6,)),
             dma((per,)),
-            dma((narrow // TILE, seq_size)),
-            dma((narrow // TILE, seq_size)),
-            dma((narrow // TILE, seq_size)),
-            dma((narrow // TILE, sources)),
-            dma((per, seq_size)),
-            dma((per, seq_size)),
+            dma((seq_size,)),
+            dma((seq_size,)),
+            dma((seq_size,)),
+            dma((sources,)),
+            dma((seq_size, per)),
+            dma((seq_size, per)),
             dma((ch_size, per)),
             dma((ch_size, per)),
         ],
@@ -430,6 +497,8 @@
         filter_taps,
         skip.reshape(1, width),
         out_weight.reshape(ch_size, width, columns),
+        jnp.asarray(forward),
+        jnp.asarray(inverse),
     )
 
 
@@ -444,12 +513,13 @@
         and lax.axis_size("ch") % 2 == 0
         and width % LANES == 0
         and block_rows % LANES == 0
-        and total // LANES % 8 == 0
+        and lax.axis_size("seq") % PAIR == 0
         and tap_rows % LANES == 0
         and total % tap_rows == 0
-        and narrow * total * LANES * 2 <= 32 * 1024 * 1024
-    )
-    chosen = toeplitz_body if fits else body
+        and tap_rows % block_rows == 0
+        and narrow * total <= 128 * 1024
+    )
+    chosen = block_body if fits else body
     return chosen(values, gates, filter_taps, skip, out_weight)
 
 

time: 32.4 us -> 29.5 us (0.910)
  the two profiles are of different devices: /device:TPU:1 before, /device:TPU:25 now
where the time goes in v1:
time: 29.5 us; the launch traced here: 29.4 us
  Pallas kernels  27.5 us (93%)
  local copies, waits for them, and re-layouts  1.87 us (6%)
    pallas_call x1, Pallas kernels, block_body(): pl.pallas_call(functools.partial(block_kernel, sources), out_shape=jax.Sh...  27.5 us
    unnamed x1, local copies, waits for them, and re-layouts  1.87 us

profile of v1, /device:TPU:25, one launch (start us, length us, event | category | flops | bytes accessed | tf_op | source)
XLA Modules:
  0.0 29.4 jit_solution(17136257507957438198)
XLA Ops:
  0.0 27.5 %shard_map.73 = f32[256,512]{1,0:T(8,128)} custom-call(f32[256,256]{1,0:T(8,128)} %values_hbm.1, f32[256,256]{1,0:T(8,128)} %gates_hbm.1, f32[512,256]{1,0:T(8,128)} %taps_hbm.1, f32[1,256]{1,0:T(1,128)} %bitcast.3, bf16[4,256,512]{2,1,0:T(8,128)(2,1)} %bitcast.2, bf16[512,256]{1,0:T(8,128)(2,1)} %constant.4.clone.forward_hbm, ...), custom_call_target="tpu_custom_call" | custom-call | tf_op jit(solution)/shard_map/pallas_call | solution.py:457
  27.5 1.9 %copy.9 = f32[256,512]{1,0:T(8,128)} copy(f32[256,512]{1,0:T(8,128)} %shard_map.73) | data formatting | bytes 1048576

commit v2 on v1

--- a/solution.py
+++ b/solution.py
@@ -134,7 +134,6 @@
 
 
 def block_kernel(
-    tap_sources,
     values_hbm,
     gates_hbm,
     taps_hbm,
@@ -170,11 +169,14 @@
     y_recv,
     g_send,
     g_recv,
+    seq_ready,
+    ch_ready,
 ):
-    seq_size, narrow, block_rows = x_out.shape
+    sources, narrow, block_rows = x_out.shape
+    seq_size = x_in.shape[0]
     tap_rows = h_out.shape[2]
-    ch_size, _, width = hidden.shape
-    per = block_rows // LANES
+    ch_size, halves, _, half_width = hidden.shape
+    per, pieces = block_rows // LANES, tap_rows // LANES
     me, lane_group = lax.axis_index("seq"), lax.axis_index("ch")
     f32, bf16 = jnp.float32, jnp.bfloat16
 
@@ -195,56 +197,58 @@
         load.start()
 
     barrier = pltpu.get_barrier_semaphore()
-    for step in range(1, seq_size):
-        pl.semaphore_signal(
-            barrier, inc=1, device_id={"seq": lax.rem(me + step, seq_size)}, device_id_type=MESH
-        )
-    for step in range(1, ch_size):
-        pl.semaphore_signal(
-            barrier, inc=1, device_id={"ch": lax.rem(lane_group + step, ch_size)}, device_id_type=MESH
+    for other in range(1, seq_size):
+        @pl.when((me < other) & (me < sources))
+        def _():
+            pl.semaphore_signal(barrier, inc=1, device_id={"seq": other}, device_id_type=MESH)
+    for other in range(1, ch_size):
+        @pl.when(lane_group < other)
+        def _():
+            pl.semaphore_signal(barrier, inc=1, device_id={"ch": other}, device_id_type=MESH)
+    earlier = jnp.minimum(me, sources) + lane_group
+
+    @pl.when(earlier > 0)
+    def _():
+        pl.semaphore_wait(barrier, earlier)
+    for other in range(sources):
+        @pl.when(me > other)
+        def _():
+            pl.semaphore_signal(
+                seq_ready.at[me], inc=1, device_id={"seq": other}, device_id_type=MESH
+            )
+    for other in range(ch_size - 1):
+        @pl.when(lane_group > other)
+        def _():
+            pl.semaphore_signal(
+                ch_ready.at[lane_group], inc=1, device_id={"ch": other}, device_id_type=MESH
+            )
+
+    def x_copy(to):
+        return pltpu.make_async_remote_copy(
+            x_out.at[to], x_in.at[me], x_send.at[to], x_recv.at[me],
+            device_id={"seq": to}, device_id_type=MESH,
+        )
+
+    def h_copy(to):
+        return pltpu.make_async_remote_copy(
+            h_out.at[to], h_in.at[me], h_send.at[to], h_recv.at[me],
+            device_id={"seq": to}, device_id_type=MESH,
+        )
+
+    def y_copy(to):
+        return pltpu.make_async_remote_copy(
+            y_out.at[to], y_in.at[me], y_send.at[to], y_recv.at[me],
+            device_id={"seq": to}, device_id_type=MESH,
         )
 
     loads[0].wait()
     x_out[...] = values_ref[...].T.astype(bf16).reshape(x_out.shape)
-    x_in[me] = x_out[me]
     loads[1].wait()
 
-    @pl.when(me < tap_sources)
+    @pl.when(me >= sources)
     def _():
-        h_out[...] = taps_ref[...].T.astype(bf16).reshape(h_out.shape)
-        h_in[me] = h_out[me]
-
-    rounds = seq_size // PAIR
-    home, side = me // PAIR, lax.rem(me, PAIR)
-    targets = []
-    for near in [rounds // 2] + [n for k in range(1, (rounds + 1) // 2) for n in (rounds - k, k)] + [0]:
-        for turn in range(PAIR):
-            if near or turn:
-                targets.append(
-                    lax.rem(home + near, rounds) * PAIR + lax.rem(side + turn, PAIR)
-                )
-
-    def x_copy(place, to):
-        return pltpu.make_async_remote_copy(
-            x_out.at[to], x_in.at[me], x_send.at[place], x_recv.at[me],
-            device_id={"seq": to}, device_id_type=MESH,
-        )
-
-    def h_copy(place, to):
-        return pltpu.make_async_remote_copy(
-            h_out.at[to], h_in.at[me], h_send.at[place], h_recv.at[me],
-            device_id={"seq": to}, device_id_type=MESH,
-        )
-
-    pl.semaphore_wait(barrier, seq_size + ch_size - 2)
-    x_copies = [x_copy(place, to) for place, to in enumerate(targets)]
-    for copy in x_copies:
-        copy.start()
-
-    @pl.when(me < tap_sources)
-    def _():
-        for place, to in enumerate(targets):
-            h_copy(place, to).start()
+        for to in range(sources):
+            x_copy(to).start()
 
     for load in loads[2:4]:
         load.wait()
@@ -256,7 +260,6 @@
                 h_out.at[0], h_in.at[source], h_send.at[0], h_recv.at[source],
                 device_id={"seq": source}, device_id_type=MESH,
             ).wait_recv()
-        pieces = tap_rows // LANES
         rows = jnp.concatenate(
             [h_in[source, :, piece * LANES : (piece + 1) * LANES] for piece in range(pieces)], axis=0
         )
@@ -276,7 +279,7 @@
             def _():
                 pltpu.make_async_remote_copy(
                     x_out.at[0], x_in.at[source], x_send.at[0], x_recv.at[source],
-                    device_id={"seq": source}, device_id_type=MESH,
+                    device_id={"seq": 0}, device_id_type=MESH,
                 ).wait_recv()
         if first:
             before = x_in[first - 1, :, block_rows - LANES :]
@@ -295,43 +298,45 @@
             PAIR * per, narrow, 2 * LANES
         )
 
-    def multiply(first):
-        start = first * per
-        count = PAIR * per
-        for part in range(narrow // TILE):
-            rows = slice(part * TILE, (part + 1) * TILE)
+    def multiply(first, low, high, fresh):
+        start, count = first * per, PAIR * per
+
+        def one(part, carry):
+            rows = pl.ds(pl.multiple_of(part * TILE, TILE), TILE)
+            real_lanes, imag_lanes = slice(0, LANES), slice(LANES, 2 * LANES)
             cache = {}
 
             def x_part(block):
                 if block not in cache:
-                    cache[block] = (x_waves[block, rows, :LANES], x_waves[block, rows, LANES:])
+                    cache[block] = (
+                        x_waves[block, rows, real_lanes], x_waves[block, rows, imag_lanes]
+                    )
                 return cache[block]
 
             sums = [None] * count
-            for lag in range(start + count):
-                h_real, h_imag = h_waves[lag, rows, :LANES], h_waves[lag, rows, LANES:]
+            if not fresh:
+                sums = [
+                    (y_waves[spot, rows, real_lanes], y_waves[spot, rows, imag_lanes])
+                    for spot in range(count)
+                ]
+            for lag in range(max(0, start - high + 1), start + count - low):
+                h_real, h_imag = h_waves[lag, rows, real_lanes], h_waves[lag, rows, imag_lanes]
                 for spot in range(count):
                     block = start + spot - lag
-                    if block < 0:
+                    if not low <= block < high:
                         continue
                     x_real, x_imag = x_part(block)
                     real = x_real * h_real - x_imag * h_imag
                     imag = x_real * h_imag + x_imag * h_real
-                    if sums[spot] is None:
-                        sums[spot] = (real, imag)
-                    else:
-                        sums[spot] = (sums[spot][0] + real, sums[spot][1] + imag)
+                    if sums[spot] is not None:
+                        real, imag = sums[spot][0] + real, sums[spot][1] + imag
+                    sums[spot] = (real, imag)
             for spot in range(count):
-                y_waves[spot, rows, :LANES] = sums[spot][0]
-                y_waves[spot, rows, LANES:] = sums[spot][1]
-
-    def y_copy(target, piece):
-        span = pl.ds(piece * LANES, LANES)
-        return pltpu.make_async_remote_copy(
-            y_out.at[target, :, span], y_in.at[me, :, span],
-            y_send.at[target, piece], y_recv.at[me, piece],
-            device_id={"seq": target}, device_id_type=MESH,
-        )
+                y_waves[spot, rows, real_lanes] = sums[spot][0]
+                y_waves[spot, rows, imag_lanes] = sums[spot][1]
+            return carry
+
+        lax.fori_loop(0, narrow // TILE, one, 0)
 
     def give_back(first):
         waves = y_waves[...].reshape(PAIR * per * narrow, 2 * LANES)
@@ -345,108 +350,130 @@
             y_out[source, :, piece * LANES : (piece + 1) * LANES] = convolved[
                 spot * narrow : (spot + 1) * narrow
             ]
-        for piece in range(per):
-            for target in range(first, first + PAIR):
-                @pl.when(me != target)
-                def _():
-                    y_copy(target, piece).start()
-
-    taken = 0
-    for first in range(0, seq_size, PAIR):
-        while taken < tap_sources and taken * tap_rows < (first + PAIR) * block_rows:
-            take_taps(taken)
-            taken += 1
-        take_values(first)
-        multiply(first)
-        give_back(first)
-    y_in[me] = y_out[me]
+        for to in range(first, first + PAIR):
+            if to >= sources:
+                pl.semaphore_wait(seq_ready.at[to], 1)
+
+            @pl.when(me != to)
+            def _():
+                y_copy(to).start()
+
+    @pl.when(me < sources)
+    def _():
+        h_out[...] = taps_ref[...].T.astype(bf16).reshape(h_out.shape)
+        for to in range(sources):
+            @pl.when(me < to)
+            def _():
+                pl.semaphore_wait(seq_ready.at[to], 1)
+
+            @pl.when(me != to)
+            def _():
+                x_copy(to).start()
+                h_copy(to).start()
+        x_in[me] = x_out[me]
+        h_in[me] = h_out[me]
+        taken = 0
+        for first in range(0, seq_size, PAIR):
+            while taken < sources and taken * tap_rows < (first + PAIR) * block_rows:
+                take_taps(taken)
+                taken += 1
+            if first:
+                multiply(first, 0, first * per, True)
+            take_values(first)
+            multiply(first, first * per, (first + PAIR) * per, not first)
+            give_back(first)
+        y_in[me] = y_out[me]
 
     partner = lane_group + 1 - 2 * lax.rem(lane_group, 2)
     pairs = ch_size // 2
-
-    def spread(kind, piece, slot, to):
-        block = hidden.at[slot, pl.ds(piece * LANES, LANES)]
+    lead = lax.rem((me // PAIR + 1) // 2, halves)
+    order = [lax.rem(lead + turn, halves) for turn in range(halves)]
+
+    def spread(kind, half, slot, to):
+        block = hidden.at[slot, half]
         copy = pltpu.make_async_remote_copy(
-            block, block, g_send.at[kind, piece], g_recv.at[kind, piece],
+            block, block, g_send.at[kind, half], g_recv.at[kind, half],
             device_id={"ch": to}, device_id_type=MESH,
         )
         copy.start()
         g_copies.append(copy)
         return copy
 
-    def add_product(piece, slot, first=False):
-        rows = slice(piece * LANES, (piece + 1) * LANES)
-        term = jnp.dot(hidden[slot, rows], weight[slot], preferred_element_type=f32)
-        out_ref[rows] = term if first else out_ref[rows] + term
+    def add_product(half, slot, first=False):
+        term = jnp.dot(hidden[slot, half], weight[slot, half], preferred_element_type=f32)
+        out_ref[...] = term if first else out_ref[...] + term
+
+    for other in range(1, ch_size):
+        @pl.when(lane_group < other)
+        def _():
+            pl.semaphore_wait(ch_ready.at[other], 1)
 
     g_copies, direct, relayed = [], {}, {}
     loads[4].wait()
-    for piece in range(per):
-        rows = slice(piece * LANES, (piece + 1) * LANES)
-        for source in range(seq_size):
+    for turn, half in enumerate(order):
+        for part in range(PAIR):
+            source = half * PAIR + part
+
             @pl.when(me != source)
             def _():
-                span = pl.ds(piece * LANES, LANES)
                 pltpu.make_async_remote_copy(
-                    y_out.at[source, :, span], y_in.at[source, :, span],
-                    y_send.at[source, piece], y_recv.at[source, piece],
-                    device_id={"seq": source}, device_id_type=MESH,
+                    y_out.at[0], y_in.at[source], y_send.at[0], y_recv.at[source],
+                    device_id={"seq": 0}, device_id_type=MESH,
                 ).wait_recv()
-        convolved = y_in[:, :, rows].astype(f32).reshape(width, LANES).T
-        hidden[lane_group, rows] = (
-            gates_ref[rows] * (convolved + skip_ref[...] * values_ref[rows])
+        convolved = y_in[pl.ds(half * PAIR, PAIR)].astype(f32).reshape(half_width, block_rows).T
+        span = pl.ds(pl.multiple_of(half * half_width, half_width), half_width)
+        hidden[lane_group, half] = (
+            gates_ref[:, span] * (convolved + skip_ref[:, span] * values_ref[:, span])
         ).astype(bf16)
         for pair in range(1, pairs):
-            direct[pair, piece] = spread(
-                2 * pair - 1, piece, lane_group, lax.rem(lane_group + 2 * pair, ch_size)
+            direct[pair, turn] = spread(
+                2 * pair - 1, half, lane_group, lax.rem(lane_group + 2 * pair, ch_size)
             )
-        direct[0, piece] = spread(0, piece, lane_group, partner)
+        direct[0, turn] = spread(0, half, lane_group, partner)
     loads[5].wait()
-    for piece in range(per):
-        add_product(piece, lane_group, True)
-    for piece in range(per):
-        direct[0, piece].wait_recv()
-        add_product(piece, partner)
-    for piece in range(per):
+    for turn, half in enumerate(order):
+        add_product(half, lane_group, not turn)
+    for turn, half in enumerate(order):
+        direct[0, turn].wait_recv()
+        add_product(half, partner)
         for pair in range(1, pairs):
             slot = lax.rem(lane_group + ch_size - 2 * pair, ch_size)
-            direct[pair, piece].wait_recv()
-            relayed[pair, piece] = spread(2 * pair, piece, slot, partner)
-            add_product(piece, slot)
-    stores = []
-    for piece in range(per):
-        rows = pl.ds(piece * LANES, LANES)
+            direct[pair, turn].wait_recv()
+            relayed[pair, turn] = spread(2 * pair, half, slot, partner)
+            add_product(half, slot)
+    for turn, half in enumerate(order):
         for pair in range(1, pairs):
             slot = lax.rem(partner + ch_size - 2 * pair, ch_size)
-            relayed[pair, piece].wait_recv()
-            add_product(piece, slot)
-        store = pltpu.make_async_copy(out_ref.at[rows], out_hbm.at[rows], out_sem.at[piece])
-        store.start()
-        stores.append(store)
-    for store in stores:
-        store.wait()
-
-    for copy in x_copies + g_copies:
+            relayed[pair, turn].wait_recv()
+            add_product(half, slot)
+    store = pltpu.make_async_copy(out_ref, out_hbm, out_sem)
+    store.start()
+    store.wait()
+
+    for copy in g_copies:
         copy.wait_send()
-    for target in range(seq_size):
-        @pl.when(me != target)
-        def _():
-            for piece in range(per):
-                y_copy(target, piece).wait_send()
-
-    @pl.when(me < tap_sources)
-    def _():
-        for place, to in enumerate(targets):
-            h_copy(place, to).wait_send()
+    for to in range(sources):
+        @pl.when(me != to)
+        def _():
+            x_copy(to).wait_send()
+
+        @pl.when((me != to) & (me < sources))
+        def _():
+            h_copy(to).wait_send()
+    for to in range(seq_size):
+        @pl.when((me != to) & (me < sources))
+        def _():
+            y_copy(to).wait_send()
 
 
 def block_body(values, gates, filter_taps, skip, out_weight):
     seq_size, ch_size = lax.axis_size("seq"), lax.axis_size("ch")
     block_rows, width = values.shape
     tap_rows = filter_taps.shape[0]
-    narrow = width // seq_size
     total = block_rows * seq_size
     sources = min(tap_rows * seq_size, total) // tap_rows
+    narrow, halves = width // sources, sources // PAIR
+    half_width = width // halves
     columns = out_weight.shape[1]
     f32, bf16 = jnp.float32, jnp.bfloat16
     vmem = pl.BlockSpec(memory_space=pltpu.VMEM)
@@ -455,7 +482,7 @@
     dma = pltpu.SemaphoreType.DMA
     forward, inverse = block_tables()
     return pl.pallas_call(
-        functools.partial(block_kernel, sources),
+        block_kernel,
         out_shape=jax.ShapeDtypeStruct((block_rows, columns), f32),
         in_specs=[hbm] * 3 + [vmem] + [hbm] * 3,
         out_specs=hbm,
@@ -464,29 +491,31 @@
             pltpu.VMEM((block_rows, width), f32),
             pltpu.VMEM((tap_rows, width), f32),
             pltpu.VMEM((block_rows, columns), f32),
-            pltpu.VMEM((seq_size, narrow, block_rows), bf16),
-            pltpu.VMEM((seq_size, narrow, tap_rows), bf16),
+            pltpu.VMEM((sources, narrow, block_rows), bf16),
+            pltpu.VMEM((sources, narrow, tap_rows), bf16),
             pltpu.VMEM((seq_size, narrow, block_rows), bf16),
             pltpu.VMEM((sources, narrow, tap_rows), bf16),
             pltpu.VMEM((total // LANES, narrow, 2 * LANES), f32),
             pltpu.VMEM((total // LANES, narrow, 2 * LANES), f32),
             pltpu.VMEM((PAIR * per, narrow, 2 * LANES), f32),
             pltpu.VMEM((seq_size, narrow, block_rows), bf16),
-            pltpu.VMEM((seq_size, narrow, block_rows), bf16),
-            pltpu.VMEM((ch_size, block_rows, width), bf16),
-            pltpu.VMEM((ch_size, width, columns), bf16),
+            pltpu.VMEM((sources, narrow, block_rows), bf16),
+            pltpu.VMEM((ch_size, halves, block_rows, half_width), bf16),
+            pltpu.VMEM((ch_size, halves, half_width, columns), bf16),
             pltpu.VMEM(forward.shape, bf16),
             pltpu.VMEM(inverse.shape, bf16),
             dma((6,)),
-            dma((per,)),
-            dma((seq_size,)),
-            dma((seq_size,)),
+            dma,
+            dma((sources,)),
             dma((seq_size,)),
             dma((sources,)),
-            dma((seq_size, per)),
-            dma((seq_size, per)),
-            dma((ch_size, per)),
-            dma((ch_size, per)),
+            dma((sources,)),
+            dma((seq_size,)),
+            dma((sources,)),
+            dma((ch_size, halves)),
+            dma((ch_size, halves)),
+            pltpu.SemaphoreType.REGULAR((seq_size,)),
+            pltpu.SemaphoreType.REGULAR((ch_size,)),
         ],
         compiler_params=pltpu.CompilerParams(
             collective_id=0, has_side_effects=True, vmem_limit_bytes=63000 * 1024
@@ -496,28 +525,29 @@
         gates,
         filter_taps,
         skip.reshape(1, width),
-        out_weight.reshape(ch_size, width, columns),
+        out_weight.reshape(ch_size, halves, half_width, columns),
         jnp.asarray(forward),
         jnp.asarray(inverse),
     )
 
 
 def local_body(values, gates, filter_taps, skip, out_weight):
-    seq_size = lax.axis_size("seq")
+    seq_size, ch_size = lax.axis_size("seq"), lax.axis_size("ch")
     block_rows, width = values.shape
     tap_rows = filter_taps.shape[0]
-    narrow = width // seq_size
     total = block_rows * seq_size
+    sources = min(tap_rows * seq_size, total) // tap_rows
     fits = (
-        width % (seq_size * TILE) == 0
-        and lax.axis_size("ch") % 2 == 0
-        and width % LANES == 0
+        sources > 0
+        and sources % PAIR == 0
+        and seq_size % PAIR == 0
+        and width % (sources * TILE) == 0
+        and width // sources * PAIR % LANES == 0
+        and ch_size % 2 == 0
         and block_rows % LANES == 0
-        and lax.axis_size("seq") % PAIR == 0
-        and tap_rows % LANES == 0
+        and tap_rows % block_rows == 0
         and total % tap_rows == 0
-        and tap_rows % block_rows == 0
-        and narrow * total <= 128 * 1024
+        and width // sources * total <= 256 * 1024
     )
     chosen = block_body if fits else body
     return chosen(values, gates, filter_taps, skip, out_weight)

time: 29.5 us -> 27.4 us (0.929)
  Pallas kernels: 27.5 us -> 25.4 us
    pallas_call x1, Pallas kernels: 27.5 us -> 25.4 us  [block_body(): pl.pallas_call(block_kernel, out_shape=jax.ShapeDtypeStruct((block_rows,...]
where the time goes in v2:
time: 27.4 us; the launch traced here: 27.3 us
  Pallas kernels  25.4 us (93%)
  local copies, waits for them, and re-layouts  1.87 us (7%)
    pallas_call x1, Pallas kernels, block_body(): pl.pallas_call(block_kernel, out_shape=jax.ShapeDtypeStruct((block_rows,...  25.4 us
    unnamed x1, local copies, waits for them, and re-layouts  1.87 us

profile of v2, /device:TPU:25, one launch (start us, length us, event | category | flops | bytes accessed | tf_op | source)
XLA Modules:
  0.0 27.3 jit_solution(12500328709539250059)
XLA Ops:
  0.0 25.4 %shard_map.73 = f32[256,512]{1,0:T(8,128)} custom-call(f32[256,256]{1,0:T(8,128)} %values_hbm.1, f32[256,256]{1,0:T(8,128)} %gates_hbm.1, f32[512,256]{1,0:T(8,128)} %taps_hbm.1, f32[1,256]{1,0:T(1,128)} %bitcast.3, bf16[4,2,128,512]{3,2,1,0:T(8,128)(2,1)} %bitcast.2, bf16[512,256]{1,0:T(8,128)(2,1)} %constant.4.clone.forward_hbm, ...), custom_call_target="tpu_custom_call" | custom-call | tf_op jit(solution)/shard_map/pallas_call | solution.py:484
  25.4 1.9 %copy.9 = f32[256,512]{1,0:T(8,128)} copy(f32[256,512]{1,0:T(8,128)} %shard_map.73) | data formatting | bytes 1048576

commit v3 on v2

--- a/solution.py
+++ b/solution.py
@@ -133,34 +133,40 @@
     return two_parts(forward, 0), two_parts(inverse, 1)
 
 
+OUTS = 4
+
+
 def block_kernel(
     values_hbm,
     gates_hbm,
     taps_hbm,
-    skip_ref,
+    skip_hbm,
     weight_hbm,
-    forward_hbm,
-    inverse_hbm,
-    out_hbm,
+    tables_hbm,
+    out_a,
+    out_b,
+    out_c,
+    out_d,
     values_ref,
     gates_ref,
     taps_ref,
-    out_ref,
+    skip_ref,
     x_out,
     h_out,
     x_in,
     h_in,
+    x_tail,
+    h_tail,
     x_waves,
     h_waves,
     y_waves,
     y_out,
+    y_tail,
     y_in,
     hidden,
     weight,
-    forward,
-    inverse,
+    tables,
     load_sem,
-    out_sem,
     x_send,
     x_recv,
     h_send,
@@ -177,6 +183,8 @@
     tap_rows = h_out.shape[2]
     ch_size, halves, _, half_width = hidden.shape
     per, pieces = block_rows // LANES, tap_rows // LANES
+    hubs, keep = sources + PAIR, narrow - TILE
+    early_taps = sources * block_rows // tap_rows
     me, lane_group = lax.axis_index("seq"), lax.axis_index("ch")
     f32, bf16 = jnp.float32, jnp.bfloat16
 
@@ -186,9 +194,9 @@
             (
                 (values_hbm, values_ref),
                 (taps_hbm, taps_ref),
-                (forward_hbm, forward),
-                (inverse_hbm, inverse),
+                (tables_hbm, tables),
                 (gates_hbm, gates_ref),
+                (skip_hbm, skip_ref),
                 (weight_hbm, weight),
             )
         )
@@ -198,19 +206,19 @@
 
     barrier = pltpu.get_barrier_semaphore()
     for other in range(1, seq_size):
-        @pl.when((me < other) & (me < sources))
+        @pl.when((me < other) & (me < hubs))
         def _():
             pl.semaphore_signal(barrier, inc=1, device_id={"seq": other}, device_id_type=MESH)
     for other in range(1, ch_size):
         @pl.when(lane_group < other)
         def _():
             pl.semaphore_signal(barrier, inc=1, device_id={"ch": other}, device_id_type=MESH)
-    earlier = jnp.minimum(me, sources) + lane_group
+    earlier = jnp.minimum(me, hubs) + lane_group
 
     @pl.when(earlier > 0)
     def _():
         pl.semaphore_wait(barrier, earlier)
-    for other in range(sources):
+    for other in range(hubs):
         @pl.when(me > other)
         def _():
             pl.semaphore_signal(
@@ -223,82 +231,140 @@
                 ch_ready.at[lane_group], inc=1, device_id={"ch": other}, device_id_type=MESH
             )
 
-    def x_copy(to):
+    forward, inverse = tables.at[: 4 * LANES], tables.at[4 * LANES :]
+    own, rest = pl.ds(0, keep), pl.ds(keep, TILE)
+
+    def transfer(source, target, sends, recvs, to, place):
         return pltpu.make_async_remote_copy(
-            x_out.at[to], x_in.at[me], x_send.at[to], x_recv.at[me],
+            source, target, sends.at[to], recvs.at[place],
             device_id={"seq": to}, device_id_type=MESH,
         )
 
-    def h_copy(to):
-        return pltpu.make_async_remote_copy(
-            h_out.at[to], h_in.at[me], h_send.at[to], h_recv.at[me],
-            device_id={"seq": to}, device_id_type=MESH,
-        )
-
-    def y_copy(to):
-        return pltpu.make_async_remote_copy(
-            y_out.at[to], y_in.at[me], y_send.at[to], y_recv.at[me],
-            device_id={"seq": to}, device_id_type=MESH,
-        )
+    def tails_of(helper):
+        return pl.ds((helper - sources) * PAIR, PAIR)
+
+    def x_copy(to, place, late):
+        if to >= sources:
+            source, target = x_out.at[tails_of(to), rest], x_tail.at[place]
+        elif late:
+            source, target = x_out.at[to, own], x_in.at[place, own]
+        else:
+            source, target = x_out.at[to], x_in.at[place]
+        return transfer(source, target, x_send, x_recv, to, place)
+
+    def h_copy(to, place, late):
+        if to >= sources:
+            source, target = h_out.at[tails_of(to), rest], h_tail.at[place]
+        elif late:
+            source, target = h_out.at[to, own], h_in.at[place, own]
+        else:
+            source, target = h_out.at[to], h_in.at[place]
+        return transfer(source, target, h_send, h_recv, to, place)
+
+    def y_copy(to, place):
+        if to >= sources:
+            source, target = y_out.at[to, own], y_in.at[place, own]
+        else:
+            source, target = y_out.at[to], y_in.at[place]
+        return transfer(source, target, y_send, y_recv, to, place)
+
+    def tail_copy(to, helper, place):
+        target = y_in.at[pl.ds((helper - sources) * PAIR, PAIR), rest]
+        return transfer(y_tail.at[to], target, y_send, y_recv, to, place)
+
+    def ready(to):
+        @pl.when(me < to)
+        def _():
+            pl.semaphore_wait(seq_ready.at[to], 1)
 
     loads[0].wait()
     x_out[...] = values_ref[...].T.astype(bf16).reshape(x_out.shape)
-    loads[1].wait()
 
     @pl.when(me >= sources)
     def _():
-        for to in range(sources):
-            x_copy(to).start()
-
-    for load in loads[2:4]:
-        load.wait()
-
-    def take_taps(source):
-        @pl.when(me != source)
-        def _():
-            pltpu.make_async_remote_copy(
-                h_out.at[0], h_in.at[source], h_send.at[0], h_recv.at[source],
-                device_id={"seq": source}, device_id_type=MESH,
-            ).wait_recv()
-        rows = jnp.concatenate(
-            [h_in[source, :, piece * LANES : (piece + 1) * LANES] for piece in range(pieces)], axis=0
+        for to in range(hubs):
+            if to >= sources:
+                ready(to)
+
+            @pl.when(me != to)
+            def _():
+                x_copy(to, me, True).start()
+
+    loads[1].wait()
+
+    @pl.when(me < sources)
+    def _():
+        h_out[...] = taps_ref[...].T.astype(bf16).reshape(h_out.shape)
+        for to in range(hubs):
+            ready(to)
+
+            @pl.when(me != to)
+            def _():
+                x_copy(to, me, False).start()
+
+            @pl.when((me != to) & (me < early_taps))
+            def _():
+                h_copy(to, me, False).start()
+
+            @pl.when((me != to) & (me >= early_taps))
+            def _():
+                h_copy(to, me, True).start()
+        x_in[me] = x_out[me]
+        h_in[me] = h_out[me]
+
+    loads[2].wait()
+
+    def take_taps(source, helper):
+        late = source >= early_taps
+        if helper:
+            h_copy(sources, source, late).wait_recv()
+            taps, count = h_tail.at[source], PAIR * TILE
+        else:
+            @pl.when(me != source)
+            def _():
+                h_copy(0, source, late).wait_recv()
+
+            taps, count = h_in.at[source], keep if late else narrow
+        rows = []
+        for piece in range(pieces):
+            lanes = slice(piece * LANES, (piece + 1) * LANES)
+            block = taps[:, :, lanes].reshape(count, LANES) if helper else taps[:count, lanes]
+            rows.append(jnp.concatenate([block, block], axis=1))
+        table = jnp.concatenate([forward[:LANES], forward[2 * LANES : 3 * LANES]], axis=0)
+        waves = jnp.dot(jnp.concatenate(rows, axis=0), table, preferred_element_type=f32)
+        h_waves[source * pieces : (source + 1) * pieces, :count] = waves.reshape(
+            pieces, count, 2 * LANES
         )
-        table = jnp.concatenate(
-            [forward[:LANES], forward[2 * LANES : 3 * LANES]], axis=0
-        )
-        waves = jnp.dot(
-            jnp.concatenate([rows, rows], axis=1), table, preferred_element_type=f32
-        )
-        h_waves[source * pieces : (source + 1) * pieces] = waves.reshape(
-            pieces, narrow, 2 * LANES
-        )
-
-    def take_values(first):
+
+    def take_values(first, helper):
+        late = first >= sources
+        count = PAIR * TILE if helper else keep if late else narrow
         for source in range(first, first + PAIR):
             @pl.when(me != source)
             def _():
-                pltpu.make_async_remote_copy(
-                    x_out.at[0], x_in.at[source], x_send.at[0], x_recv.at[source],
-                    device_id={"seq": 0}, device_id_type=MESH,
-                ).wait_recv()
-        if first:
-            before = x_in[first - 1, :, block_rows - LANES :]
-        else:
-            before = jnp.zeros((narrow, LANES), bf16)
+                x_copy(sources if helper else 0, source, late).wait_recv()
+
+        def piece_of(source, piece):
+            lanes = slice(piece * LANES, (piece + 1) * LANES)
+            if helper:
+                return x_tail[source, :, :, lanes].reshape(count, LANES)
+            return x_in[source, :count, lanes]
+
+        before = piece_of(first - 1, per - 1) if first else jnp.zeros((count, LANES), bf16)
         rows = []
         for source in range(first, first + PAIR):
             for piece in range(per):
-                here = x_in[source, :, piece * LANES : (piece + 1) * LANES]
+                here = piece_of(source, piece)
                 rows.append(jnp.concatenate([before, here, before, here], axis=1))
                 before = here
         waves = jnp.dot(
             jnp.concatenate(rows, axis=0), forward[...], preferred_element_type=f32
         )
-        x_waves[first * per : (first + PAIR) * per] = waves.reshape(
-            PAIR * per, narrow, 2 * LANES
+        x_waves[first * per : (first + PAIR) * per, :count] = waves.reshape(
+            PAIR * per, count, 2 * LANES
         )
 
-    def multiply(first, low, high, fresh):
+    def multiply(first, low, high, fresh, tiles):
         start, count = first * per, PAIR * per
 
         def one(part, carry):
@@ -316,7 +382,7 @@
             sums = [None] * count
             if not fresh:
                 sums = [
-                    (y_waves[spot, rows, real_lanes], y_waves[spot, rows, imag_lanes])
+                    (y_waves[start + spot, rows, real_lanes], y_waves[start + spot, rows, imag_lanes])
                     for spot in range(count)
                 ]
             for lag in range(max(0, start - high + 1), start + count - low):
@@ -332,61 +398,90 @@
                         real, imag = sums[spot][0] + real, sums[spot][1] + imag
                     sums[spot] = (real, imag)
             for spot in range(count):
-                y_waves[spot, rows, real_lanes] = sums[spot][0]
-                y_waves[spot, rows, imag_lanes] = sums[spot][1]
+                y_waves[start + spot, rows, real_lanes] = sums[spot][0]
+                y_waves[start + spot, rows, imag_lanes] = sums[spot][1]
             return carry
 
-        lax.fori_loop(0, narrow // TILE, one, 0)
-
-    def give_back(first):
-        waves = y_waves[...].reshape(PAIR * per * narrow, 2 * LANES)
+        lax.fori_loop(0, tiles, one, 0)
+
+    def give_back(first, helper):
+        count = PAIR * TILE if helper else keep if first >= sources else narrow
+        waves = y_waves[first * per : (first + PAIR) * per, :count].reshape(
+            PAIR * per * count, 2 * LANES
+        )
         high = waves.astype(bf16)
         low = (waves - high.astype(f32)).astype(bf16)
         both = jnp.dot(high, inverse[...], preferred_element_type=f32)
-        rest = jnp.dot(low, inverse[:, :LANES], preferred_element_type=f32)
-        convolved = (both[:, :LANES] + both[:, LANES:] + rest).astype(bf16)
+        more = jnp.dot(low, inverse[:, :LANES], preferred_element_type=f32)
+        convolved = (both[:, :LANES] + both[:, LANES:] + more).astype(bf16)
         for spot in range(PAIR * per):
-            source, piece = first + spot // per, spot % per
-            y_out[source, :, piece * LANES : (piece + 1) * LANES] = convolved[
-                spot * narrow : (spot + 1) * narrow
-            ]
+            to, piece = first + spot // per, spot % per
+            lanes = slice(piece * LANES, (piece + 1) * LANES)
+            part = convolved[spot * count : (spot + 1) * count]
+            if helper:
+                y_tail[to, :, :, lanes] = part.reshape(PAIR, TILE, LANES)
+            else:
+                y_out[to, :count, lanes] = part
         for to in range(first, first + PAIR):
-            if to >= sources:
+            if to >= hubs:
                 pl.semaphore_wait(seq_ready.at[to], 1)
-
-            @pl.when(me != to)
-            def _():
-                y_copy(to).start()
+            if not helper:
+                @pl.when(me != to)
+                def _():
+                    y_copy(to, me).start()
+            else:
+                for which in range(sources, hubs):
+                    @pl.when((me == which) & (me != to))
+                    def _():
+                        tail_copy(to, which, me).start()
+
+    def convolve(helper):
+        tiles = PAIR if helper else narrow // TILE
+        for source in range(sources):
+            if source < early_taps:
+                take_taps(source, helper)
+        for first in range(0, sources, PAIR):
+            take_values(first, helper)
+            if not helper:
+                multiply(first, 0, (first + PAIR) * per, True, tiles)
+                give_back(first, helper)
+        if not helper:
+            tiles = keep // TILE
+        for source in range(early_taps, sources):
+            take_taps(source, helper)
+        for first in range(sources, seq_size, PAIR):
+            multiply(first, 0, sources * per, True, tiles)
+        for fresh in range(sources, seq_size, PAIR):
+            take_values(fresh, helper)
+            multiply(fresh, fresh * per, (fresh + PAIR) * per, False, tiles)
+            give_back(fresh, helper)
+            for first in range(fresh + PAIR, seq_size, PAIR):
+                multiply(first, fresh * per, (fresh + PAIR) * per, False, tiles)
 
     @pl.when(me < sources)
     def _():
-        h_out[...] = taps_ref[...].T.astype(bf16).reshape(h_out.shape)
-        for to in range(sources):
-            @pl.when(me < to)
-            def _():
-                pl.semaphore_wait(seq_ready.at[to], 1)
-
-            @pl.when(me != to)
-            def _():
-                x_copy(to).start()
-                h_copy(to).start()
-        x_in[me] = x_out[me]
-        h_in[me] = h_out[me]
-        taken = 0
-        for first in range(0, seq_size, PAIR):
-            while taken < sources and taken * tap_rows < (first + PAIR) * block_rows:
-                take_taps(taken)
-                taken += 1
-            if first:
-                multiply(first, 0, first * per, True)
-            take_values(first)
-            multiply(first, first * per, (first + PAIR) * per, not first)
-            give_back(first)
+        convolve(False)
         y_in[me] = y_out[me]
+
+    for which in range(sources, hubs):
+        @pl.when(me == which)
+        def _():
+            tails = slice((which - sources) * PAIR, (which - sources + 1) * PAIR)
+            x_tail[which] = x_out[tails, keep:]
+
+    @pl.when((me >= sources) & (me < hubs))
+    def _():
+        convolve(True)
+
+    for which in range(sources, hubs):
+        @pl.when(me == which)
+        def _():
+            tails = slice((which - sources) * PAIR, (which - sources + 1) * PAIR)
+            y_in[tails, keep:] = y_tail[which]
 
     partner = lane_group + 1 - 2 * lax.rem(lane_group, 2)
     pairs = ch_size // 2
-    lead = lax.rem((me // PAIR + 1) // 2, halves)
+    lead = jnp.minimum(me // PAIR, halves - 1)
     order = [lax.rem(lead + turn, halves) for turn in range(halves)]
 
     def spread(kind, half, slot, to):
@@ -401,25 +496,35 @@
 
     def add_product(half, slot, first=False):
         term = jnp.dot(hidden[slot, half], weight[slot, half], preferred_element_type=f32)
-        out_ref[...] = term if first else out_ref[...] + term
+        for place, out in enumerate(outs):
+            part = term[place * out_rows : (place + 1) * out_rows]
+            out[...] = part if first else out[...] + part
 
     for other in range(1, ch_size):
         @pl.when(lane_group < other)
         def _():
             pl.semaphore_wait(ch_ready.at[other], 1)
 
+    outs = (out_a, out_b, out_c, out_d)
+    out_rows = out_a.shape[0]
     g_copies, direct, relayed = [], {}, {}
-    loads[4].wait()
+    for load in loads[3:5]:
+        load.wait()
     for turn, half in enumerate(order):
         for part in range(PAIR):
             source = half * PAIR + part
 
-            @pl.when(me != source)
-            def _():
-                pltpu.make_async_remote_copy(
-                    y_out.at[0], y_in.at[source], y_send.at[0], y_recv.at[source],
-                    device_id={"seq": 0}, device_id_type=MESH,
-                ).wait_recv()
+            @pl.when((me != source) & (me < sources))
+            def _():
+                y_copy(0, source).wait_recv()
+
+            @pl.when(me >= sources)
+            def _():
+                y_copy(sources, source).wait_recv()
+
+        @pl.when((me >= sources) & (me != sources + half))
+        def _():
+            tail_copy(sources, sources, sources + half).wait_recv()
         convolved = y_in[pl.ds(half * PAIR, PAIR)].astype(f32).reshape(half_width, block_rows).T
         span = pl.ds(pl.multiple_of(half * half_width, half_width), half_width)
         hidden[lane_group, half] = (
@@ -446,24 +551,27 @@
             slot = lax.rem(partner + ch_size - 2 * pair, ch_size)
             relayed[pair, turn].wait_recv()
             add_product(half, slot)
-    store = pltpu.make_async_copy(out_ref, out_hbm, out_sem)
-    store.start()
-    store.wait()
 
     for copy in g_copies:
         copy.wait_send()
-    for to in range(sources):
-        @pl.when(me != to)
-        def _():
-            x_copy(to).wait_send()
-
-        @pl.when((me != to) & (me < sources))
-        def _():
-            h_copy(to).wait_send()
+    for to in range(hubs):
+        for late in (False, True):
+            @pl.when((me != to) & ((me >= sources) == late))
+            def _():
+                x_copy(to, me, late).wait_send()
+
+            @pl.when((me != to) & (me < sources) & ((me >= early_taps) == late))
+            def _():
+                h_copy(to, me, late).wait_send()
     for to in range(seq_size):
         @pl.when((me != to) & (me < sources))
         def _():
-            y_copy(to).wait_send()
+            y_copy(to, me).wait_send()
+
+        if to >= sources:
+            @pl.when((me != to) & (me >= sources) & (me < hubs))
+            def _():
+                tail_copy(to, sources, me).wait_send()
 
 
 def block_body(values, gates, filter_taps, skip, out_weight):
@@ -472,53 +580,52 @@
     tap_rows = filter_taps.shape[0]
     total = block_rows * seq_size
     sources = min(tap_rows * seq_size, total) // tap_rows
-    narrow, halves = width // sources, sources // PAIR
+    narrow, halves, hubs = width // sources, sources // PAIR, sources + PAIR
     half_width = width // halves
     columns = out_weight.shape[1]
     f32, bf16 = jnp.float32, jnp.bfloat16
-    vmem = pl.BlockSpec(memory_space=pltpu.VMEM)
     hbm = pl.BlockSpec(memory_space=pl.ANY)
-    per = block_rows // LANES
     dma = pltpu.SemaphoreType.DMA
-    forward, inverse = block_tables()
-    return pl.pallas_call(
+    tables = np.concatenate(block_tables(), axis=0)
+    outs = pl.pallas_call(
         block_kernel,
-        out_shape=jax.ShapeDtypeStruct((block_rows, columns), f32),
-        in_specs=[hbm] * 3 + [vmem] + [hbm] * 3,
-        out_specs=hbm,
+        out_shape=[jax.ShapeDtypeStruct((block_rows // OUTS, columns), f32)] * OUTS,
+        in_specs=[hbm] * 6,
+        out_specs=[pl.BlockSpec(memory_space=pltpu.VMEM)] * OUTS,
         scratch_shapes=[
             pltpu.VMEM((block_rows, width), f32),
             pltpu.VMEM((block_rows, width), f32),
             pltpu.VMEM((tap_rows, width), f32),
-            pltpu.VMEM((block_rows, columns), f32),
+            pltpu.VMEM((1, width), f32),
             pltpu.VMEM((sources, narrow, block_rows), bf16),
             pltpu.VMEM((sources, narrow, tap_rows), bf16),
             pltpu.VMEM((seq_size, narrow, block_rows), bf16),
             pltpu.VMEM((sources, narrow, tap_rows), bf16),
+            pltpu.VMEM((seq_size, PAIR, TILE, block_rows), bf16),
+            pltpu.VMEM((sources, PAIR, TILE, tap_rows), bf16),
             pltpu.VMEM((total // LANES, narrow, 2 * LANES), f32),
             pltpu.VMEM((total // LANES, narrow, 2 * LANES), f32),
-            pltpu.VMEM((PAIR * per, narrow, 2 * LANES), f32),
+            pltpu.VMEM((total // LANES, narrow, 2 * LANES), f32),
             pltpu.VMEM((seq_size, narrow, block_rows), bf16),
+            pltpu.VMEM((seq_size, PAIR, TILE, block_rows), bf16),
             pltpu.VMEM((sources, narrow, block_rows), bf16),
             pltpu.VMEM((ch_size, halves, block_rows, half_width), bf16),
             pltpu.VMEM((ch_size, halves, half_width, columns), bf16),
-            pltpu.VMEM(forward.shape, bf16),
-            pltpu.VMEM(inverse.shape, bf16),
+            pltpu.VMEM(tables.shape, bf16),
             dma((6,)),
-            dma,
+            dma((hubs,)),
+            dma((seq_size,)),
+            dma((hubs,)),
             dma((sources,)),
             dma((seq_size,)),
-            dma((sources,)),
-            dma((sources,)),
-            dma((seq_size,)),
-            dma((sources,)),
+            dma((hubs,)),
             dma((ch_size, halves)),
             dma((ch_size, halves)),
             pltpu.SemaphoreType.REGULAR((seq_size,)),
             pltpu.SemaphoreType.REGULAR((ch_size,)),
         ],
         compiler_params=pltpu.CompilerParams(
-            collective_id=0, has_side_effects=True, vmem_limit_bytes=63000 * 1024
+            collective_id=0, has_side_effects=True, vmem_limit_bytes=54500*1024
         ),
     )(
         values,
@@ -526,9 +633,9 @@
         filter_taps,
         skip.reshape(1, width),
         out_weight.reshape(ch_size, halves, half_width, columns),
-        jnp.asarray(forward),
-        jnp.asarray(inverse),
-    )
+        jnp.asarray(tables),
+    )
+    return jnp.concatenate(outs, axis=0)
 
 
 def local_body(values, gates, filter_taps, skip, out_weight):
@@ -538,14 +645,16 @@
     total = block_rows * seq_size
     sources = min(tap_rows * seq_size, total) // tap_rows
     fits = (
-        sources > 0
-        and sources % PAIR == 0
+        sources == PAIR * PAIR
         and seq_size % PAIR == 0
+        and seq_size >= sources + PAIR
         and width % (sources * TILE) == 0
+        and width // sources > TILE
         and width // sources * PAIR % LANES == 0
         and ch_size % 2 == 0
         and block_rows % LANES == 0
         and tap_rows % block_rows == 0
+        and sources * block_rows % tap_rows == 0
         and total % tap_rows == 0
         and width // sources * total <= 256 * 1024
     )

time: 27.4 us -> 24.9 us (0.909)
  Pallas kernels: 25.4 us -> 23.2 us
  local copies, waits for them, and re-layouts: 1.87 us -> 0.68 us
  other arithmetic: 0 us -> 0.83 us
    pallas_call x1, Pallas kernels: 25.4 us -> 23.2 us  [block_body(): pl.pallas_call(block_kernel, out_shape=[jax.ShapeDtypeStruct((block_rows...]
    unnamed x1 -> x2, local copies, waits for them, and re-layouts: 1.87 us -> 0.68 us
    concatenate x0 -> x1, other arithmetic: none -> 0.83 us  [block_body(): return jnp.concatenate(outs, axis=0)]
where the time goes in v3:
time: 24.9 us; the launch traced here: 24.7 us
  Pallas kernels  23.2 us (93%)
  other arithmetic  0.83 us (3%)
  local copies, waits for them, and re-layouts  0.68 us (3%)
    pallas_call x1, Pallas kernels, block_body(): pl.pallas_call(block_kernel, out_shape=[jax.ShapeDtypeStruct((block_rows...  23.2 us
    concatenate x1, other arithmetic, block_body(): return jnp.concatenate(outs, axis=0)  0.83 us
    unnamed x2, local copies, waits for them, and re-layouts  0.68 us

profile of v3, /device:TPU:25, one launch (start us, length us, event | category | flops | bytes accessed | tf_op | source)
XLA Modules:
  0.0 24.7 jit_solution(673192893742044966)
XLA Ops:
  0.0 0.0 copy-start
  0.0 0.7 %copy-done = f32[256]{0:T(256)S(1)} copy-done((f32[256]{0:T(256)S(1)}, f32[256]{0:T(256)}, u32[]{:S(2)}) %copy-start) | copy-done | bytes 1048
  0.7 23.2 %shard_map.64 = (f32[64,512]{1,0:T(8,128)S(1)}, f32[64,512]{1,0:T(8,128)S(1)}, f32[64,512]{1,0:T(8,128)S(1)}, f32[64,512]{1,0:T(8,128)S(1)}) custom-call(f32[256,256]{1,0:T(8,128)} %values_hbm.1, f32[256,256]{1,0:T(8,128)} %gates_hbm.1, f32[512,256]{1,0:T(8,128)} %taps_hbm.1, f32[1,256]{1,0:T(1,128)S(1)} %bitcast.2, bf16[4,2,128,512]{3,2,1,0:T(8,128)(2,1)} %bitcast.3, ...), custom_call_target="tpu_custom_call" | custom-call | tf_op jit(solution)/shard_map/pallas_call | solution.py:590
  23.9 0.8 %pad_maximum_fusion = f32[256,512]{1,0:T(8,128)} fusion(f32[64,512]{1,0:T(8,128)S(1)} %get-tuple-element.12, f32[64,512]{1,0:T(8,128)S(1)} %get-tuple-element.11, f32[64,512]{1,0:T(8,128)S(1)} %get-tuple-element.10, f32[64,512]{1,0:T(8,128)S(1)} %get-tuple-element.9), kind=kLoop, calls=%fused_computation | loop fusion | flops 393216 | bytes 1048576 | tf_op jit(solution)/shard_map/concatenate | solution.py:638
Async XLA Ops:
  0.0 0.7 %copy-start = (f32[256]{0:T(256)S(1)}, f32[256]{0:T(256)}, u32[]{:S(2)}) copy-start(f32[256]{0:T(256)} %param.9) | copy-start | bytes 3076

commit v4 on v3

--- a/solution.py
+++ b/solution.py
@@ -481,8 +481,6 @@
 
     partner = lane_group + 1 - 2 * lax.rem(lane_group, 2)
     pairs = ch_size // 2
-    lead = jnp.minimum(me // PAIR, halves - 1)
-    order = [lax.rem(lead + turn, halves) for turn in range(halves)]
 
     def spread(kind, half, slot, to):
         block = hidden.at[slot, half]
@@ -510,7 +508,7 @@
     g_copies, direct, relayed = [], {}, {}
     for load in loads[3:5]:
         load.wait()
-    for turn, half in enumerate(order):
+    for half in range(halves):
         for part in range(PAIR):
             source = half * PAIR + part
 
@@ -525,31 +523,36 @@
         @pl.when((me >= sources) & (me != sources + half))
         def _():
             tail_copy(sources, sources, sources + half).wait_recv()
-        convolved = y_in[pl.ds(half * PAIR, PAIR)].astype(f32).reshape(half_width, block_rows).T
-        span = pl.ds(pl.multiple_of(half * half_width, half_width), half_width)
+        convolved = y_in[half * PAIR : (half + 1) * PAIR].astype(f32).reshape(half_width, block_rows).T
+        span = slice(half * half_width, (half + 1) * half_width)
         hidden[lane_group, half] = (
             gates_ref[:, span] * (convolved + skip_ref[:, span] * values_ref[:, span])
         ).astype(bf16)
         for pair in range(1, pairs):
-            direct[pair, turn] = spread(
+            direct[pair, half] = spread(
                 2 * pair - 1, half, lane_group, lax.rem(lane_group + 2 * pair, ch_size)
             )
-        direct[0, turn] = spread(0, half, lane_group, partner)
+            if half == halves - 1:
+                relayed[pair, half] = spread(
+                    2 * pair, half, lane_group, lax.rem(partner + 2 * pair, ch_size)
+                )
+        direct[0, half] = spread(0, half, lane_group, partner)
     loads[5].wait()
-    for turn, half in enumerate(order):
-        add_product(half, lane_group, not turn)
-    for turn, half in enumerate(order):
-        direct[0, turn].wait_recv()
+    for half in range(halves):
+        add_product(half, lane_group, not half)
+    for half in range(halves):
+        direct[0, half].wait_recv()
         add_product(half, partner)
         for pair in range(1, pairs):
             slot = lax.rem(lane_group + ch_size - 2 * pair, ch_size)
-            direct[pair, turn].wait_recv()
-            relayed[pair, turn] = spread(2 * pair, half, slot, partner)
+            direct[pair, half].wait_recv()
+            if half < halves - 1:
+                relayed[pair, half] = spread(2 * pair, half, slot, partner)
             add_product(half, slot)
-    for turn, half in enumerate(order):
+    for half in range(halves):
         for pair in range(1, pairs):
             slot = lax.rem(partner + ch_size - 2 * pair, ch_size)
-            relayed[pair, turn].wait_recv()
+            relayed[pair, half].wait_recv()
             add_product(half, slot)
 
     for copy in g_copies:
@@ -625,7 +628,7 @@
             pltpu.SemaphoreType.REGULAR((ch_size,)),
         ],
         compiler_params=pltpu.CompilerParams(
-            collective_id=0, has_side_effects=True, vmem_limit_bytes=54500*1024
+            collective_id=0, has_side_effects=True, vmem_limit_bytes=54500 * 1024
         ),
     )(
         values,

time: 24.9 us -> 23.5 us (0.944)
  Pallas kernels: 23.2 us -> 21.8 us
    pallas_call x1, Pallas kernels: 23.2 us -> 21.8 us  [block_body(): pl.pallas_call(block_kernel, out_shape=[jax.ShapeDtypeStruct((block_rows...]
where the time goes in v4:
time: 23.5 us; the launch traced here: 23.3 us
  Pallas kernels  21.8 us (93%)
  other arithmetic  0.83 us (4%)
  local copies, waits for them, and re-layouts  0.68 us (3%)
    pallas_call x1, Pallas kernels, block_body(): pl.pallas_call(block_kernel, out_shape=[jax.ShapeDtypeStruct((block_rows...  21.8 us
    concatenate x1, other arithmetic, block_body(): return jnp.concatenate(outs, axis=0)  0.83 us
    unnamed x2, local copies, waits for them, and re-layouts  0.68 us

profile of v4, /device:TPU:25, one launch (start us, length us, event | category | flops | bytes accessed | tf_op | source)
XLA Modules:
  0.0 23.3 jit_solution(11557890832348081463)
XLA Ops:
  0.0 0.0 copy-start
  0.0 0.7 %copy-done = f32[256]{0:T(256)S(1)} copy-done((f32[256]{0:T(256)S(1)}, f32[256]{0:T(256)}, u32[]{:S(2)}) %copy-start) | copy-done | bytes 1048
  0.7 21.8 %shard_map.64 = (f32[64,512]{1,0:T(8,128)S(1)}, f32[64,512]{1,0:T(8,128)S(1)}, f32[64,512]{1,0:T(8,128)S(1)}, f32[64,512]{1,0:T(8,128)S(1)}) custom-call(f32[256,256]{1,0:T(8,128)} %values_hbm.1, f32[256,256]{1,0:T(8,128)} %gates_hbm.1, f32[512,256]{1,0:T(8,128)} %taps_hbm.1, f32[1,256]{1,0:T(1,128)S(1)} %bitcast.2, bf16[4,2,128,512]{3,2,1,0:T(8,128)(2,1)} %bitcast.3, ...), custom_call_target="tpu_custom_call" | custom-call | tf_op jit(solution)/shard_map/pallas_call | solution.py:593
  22.5 0.8 %pad_maximum_fusion = f32[256,512]{1,0:T(8,128)} fusion(f32[64,512]{1,0:T(8,128)S(1)} %get-tuple-element.12, f32[64,512]{1,0:T(8,128)S(1)} %get-tuple-element.11, f32[64,512]{1,0:T(8,128)S(1)} %get-tuple-element.10, f32[64,512]{1,0:T(8,128)S(1)} %get-tuple-element.9), kind=kLoop, calls=%fused_computation | loop fusion | flops 393216 | bytes 1048576 | tf_op jit(solution)/shard_map/concatenate | solution.py:641
Async XLA Ops:
  0.0 0.7 %copy-start = (f32[256]{0:T(256)S(1)}, f32[256]{0:T(256)}, u32[]{:S(2)}) copy-start(f32[256]{0:T(256)} %param.9) | copy-start | bytes 3076

commit v5 on v4

--- a/solution.py
+++ b/solution.py
@@ -277,6 +277,12 @@
         def _():
             pl.semaphore_wait(seq_ready.at[to], 1)
 
+    def send_tails():
+        for to in range(sources, hubs):
+            pl.semaphore_wait(seq_ready.at[to], 1)
+            x_copy(to, me, False).start()
+            h_copy(to, me, False).start()
+
     loads[0].wait()
     x_out[...] = values_ref[...].T.astype(bf16).reshape(x_out.shape)
 
@@ -295,7 +301,7 @@
     @pl.when(me < sources)
     def _():
         h_out[...] = taps_ref[...].T.astype(bf16).reshape(h_out.shape)
-        for to in range(hubs):
+        for to in range(sources):
             ready(to)
 
             @pl.when(me != to)
@@ -309,22 +315,36 @@
             @pl.when((me != to) & (me >= early_taps))
             def _():
                 h_copy(to, me, True).start()
+
+        @pl.when(me >= early_taps)
+        def _():
+            send_tails()
+
         x_in[me] = x_out[me]
         h_in[me] = h_out[me]
 
     loads[2].wait()
 
-    def take_taps(source, helper):
+    def wait_taps(source, helper):
         late = source >= early_taps
         if helper:
             h_copy(sources, source, late).wait_recv()
+        else:
+            @pl.when(me != source)
+            def _():
+                h_copy(0, source, late).wait_recv()
+
+    def wait_values(first, helper):
+        for source in range(first, first + PAIR):
+            @pl.when(me != source)
+            def _():
+                x_copy(sources if helper else 0, source, first >= sources).wait_recv()
+
+    def take_taps(source, helper):
+        if helper:
             taps, count = h_tail.at[source], PAIR * TILE
         else:
-            @pl.when(me != source)
-            def _():
-                h_copy(0, source, late).wait_recv()
-
-            taps, count = h_in.at[source], keep if late else narrow
+            taps, count = h_in.at[source], keep if source >= early_taps else narrow
         rows = []
         for piece in range(pieces):
             lanes = slice(piece * LANES, (piece + 1) * LANES)
@@ -339,11 +359,6 @@
     def take_values(first, helper):
         late = first >= sources
         count = PAIR * TILE if helper else keep if late else narrow
-        for source in range(first, first + PAIR):
-            @pl.when(me != source)
-            def _():
-                x_copy(sources if helper else 0, source, late).wait_recv()
-
         def piece_of(source, piece):
             lanes = slice(piece * LANES, (piece + 1) * LANES)
             if helper:
@@ -435,32 +450,61 @@
                     def _():
                         tail_copy(to, which, me).start()
 
-    def convolve(helper):
-        tiles = PAIR if helper else narrow // TILE
-        for source in range(sources):
-            if source < early_taps:
-                take_taps(source, helper)
+    def convolve_own():
+        taken = 0
         for first in range(0, sources, PAIR):
-            take_values(first, helper)
-            if not helper:
-                multiply(first, 0, (first + PAIR) * per, True, tiles)
-                give_back(first, helper)
-        if not helper:
-            tiles = keep // TILE
+            fresh = taken
+            while taken < early_taps and taken * tap_rows < (first + PAIR) * block_rows:
+                wait_taps(taken, False)
+                taken += 1
+            wait_values(first, False)
+            if not first:
+                @pl.when(me < early_taps)
+                def _():
+                    send_tails()
+
+            for source in range(fresh, taken):
+                take_taps(source, False)
+            take_values(first, False)
+            multiply(first, 0, (first + PAIR) * per, True, narrow // TILE)
+            give_back(first, False)
+        tiles = keep // TILE
         for source in range(early_taps, sources):
-            take_taps(source, helper)
+            wait_taps(source, False)
+        for source in range(early_taps, sources):
+            take_taps(source, False)
         for first in range(sources, seq_size, PAIR):
             multiply(first, 0, sources * per, True, tiles)
-        for fresh in range(sources, seq_size, PAIR):
-            take_values(fresh, helper)
-            multiply(fresh, fresh * per, (fresh + PAIR) * per, False, tiles)
-            give_back(fresh, helper)
-            for first in range(fresh + PAIR, seq_size, PAIR):
-                multiply(first, fresh * per, (fresh + PAIR) * per, False, tiles)
+        for first in range(sources, seq_size, PAIR):
+            wait_values(first, False)
+        for first in range(sources, seq_size, PAIR):
+            take_values(first, False)
+        for first in range(sources, seq_size, PAIR):
+            multiply(first, sources * per, (first + PAIR) * per, False, tiles)
+            give_back(first, False)
+
+    def convolve_tails():
+        for first in range(PAIR, seq_size, PAIR):
+            wait_values(first, True)
+            if first >= sources:
+                take_values(first, True)
+        for source in range(early_taps, sources):
+            wait_taps(source, True)
+            take_taps(source, True)
+        wait_values(0, True)
+        for source in range(early_taps):
+            wait_taps(source, True)
+        for first in range(0, sources, PAIR):
+            take_values(first, True)
+        for source in range(early_taps):
+            take_taps(source, True)
+        for first in range(sources, seq_size, PAIR):
+            multiply(first, 0, (first + PAIR) * per, True, PAIR)
+            give_back(first, True)
 
     @pl.when(me < sources)
     def _():
-        convolve(False)
+        convolve_own()
         y_in[me] = y_out[me]
 
     for which in range(sources, hubs):
@@ -471,7 +515,7 @@
 
     @pl.when((me >= sources) & (me < hubs))
     def _():
-        convolve(True)
+        convolve_tails()
 
     for which in range(sources, hubs):
         @pl.when(me == which)

time: 23.5 us -> 22.9 us (0.974)
  Pallas kernels: 21.8 us -> 21.3 us
    pallas_call x1, Pallas kernels: 21.8 us -> 21.3 us  [block_body(): pl.pallas_call(block_kernel, out_shape=[jax.ShapeDtypeStruct((block_rows...]
where the time goes in v5:
time: 22.9 us; the launch traced here: 22.8 us
  Pallas kernels  21.3 us (93%)
  other arithmetic  0.83 us (4%)
  local copies, waits for them, and re-layouts  0.68 us (3%)
    pallas_call x1, Pallas kernels, block_body(): pl.pallas_call(block_kernel, out_shape=[jax.ShapeDtypeStruct((block_rows...  21.3 us
    concatenate x1, other arithmetic, block_body(): return jnp.concatenate(outs, axis=0)  0.83 us
    unnamed x2, local copies, waits for them, and re-layouts  0.68 us

profile of v5, /device:TPU:25, one launch (start us, length us, event | category | flops | bytes accessed | tf_op | source)
XLA Modules:
  0.0 22.8 jit_solution(2010056228644549651)
XLA Ops:
  0.0 0.0 copy-start
  0.0 0.7 %copy-done = f32[256]{0:T(256)S(1)} copy-done((f32[256]{0:T(256)S(1)}, f32[256]{0:T(256)}, u32[]{:S(2)}) %copy-start) | copy-done | bytes 1048
  0.7 21.3 %shard_map.64 = (f32[64,512]{1,0:T(8,128)S(1)}, f32[64,512]{1,0:T(8,128)S(1)}, f32[64,512]{1,0:T(8,128)S(1)}, f32[64,512]{1,0:T(8,128)S(1)}) custom-call(f32[256,256]{1,0:T(8,128)} %values_hbm.1, f32[256,256]{1,0:T(8,128)} %gates_hbm.1, f32[512,256]{1,0:T(8,128)} %taps_hbm.1, f32[1,256]{1,0:T(1,128)S(1)} %bitcast.2, bf16[4,2,128,512]{3,2,1,0:T(8,128)(2,1)} %bitcast.3, ...), custom_call_target="tpu_custom_call" | custom-call | tf_op jit(solution)/shard_map/pallas_call | solution.py:637
  22.0 0.8 %pad_maximum_fusion = f32[256,512]{1,0:T(8,128)} fusion(f32[64,512]{1,0:T(8,128)S(1)} %get-tuple-element.12, f32[64,512]{1,0:T(8,128)S(1)} %get-tuple-element.11, f32[64,512]{1,0:T(8,128)S(1)} %get-tuple-element.10, f32[64,512]{1,0:T(8,128)S(1)} %get-tuple-element.9), kind=kLoop, calls=%fused_computation | loop fusion | flops 393216 | bytes 1048576 | tf_op jit(solution)/shard_map/concatenate | solution.py:685
Async XLA Ops:
  0.0 0.7 %copy-start = (f32[256]{0:T(256)S(1)}, f32[256]{0:T(256)}, u32[]{:S(2)}) copy-start(f32[256]{0:T(256)} %param.9) | copy-start | bytes 3076

commit v6 on v5

--- a/solution.py
+++ b/solution.py
@@ -498,7 +498,7 @@
             take_values(first, True)
         for source in range(early_taps):
             take_taps(source, True)
-        for first in range(sources, seq_size, PAIR):
+        for first in range(seq_size - PAIR, sources - 1, -PAIR):
             multiply(first, 0, (first + PAIR) * per, True, PAIR)
             give_back(first, True)
 

time: 22.9 us -> 22.8 us (level)
  no operation moved by 1% of the time
where the time goes in v6:
time: 22.8 us; the launch traced here: 22.7 us
  Pallas kernels  21.2 us (93%)
  other arithmetic  0.83 us (4%)
  local copies, waits for them, and re-layouts  0.68 us (3%)
    pallas_call x1, Pallas kernels, block_body(): pl.pallas_call(block_kernel, out_shape=[jax.ShapeDtypeStruct((block_rows...  21.2 us
    concatenate x1, other arithmetic, block_body(): return jnp.concatenate(outs, axis=0)  0.83 us
    unnamed x2, local copies, waits for them, and re-layouts  0.68 us

profile of v6, /device:TPU:25, one launch (start us, length us, event | category | flops | bytes accessed | tf_op | source)
XLA Modules:
  0.0 22.7 jit_solution(3780522818768168327)
XLA Ops:
  0.0 0.0 copy-start
  0.0 0.7 %copy-done = f32[256]{0:T(256)S(1)} copy-done((f32[256]{0:T(256)S(1)}, f32[256]{0:T(256)}, u32[]{:S(2)}) %copy-start) | copy-done | bytes 1048
  0.7 21.2 %shard_map.64 = (f32[64,512]{1,0:T(8,128)S(1)}, f32[64,512]{1,0:T(8,128)S(1)}, f32[64,512]{1,0:T(8,128)S(1)}, f32[64,512]{1,0:T(8,128)S(1)}) custom-call(f32[256,256]{1,0:T(8,128)} %values_hbm.1, f32[256,256]{1,0:T(8,128)} %gates_hbm.1, f32[512,256]{1,0:T(8,128)} %taps_hbm.1, f32[1,256]{1,0:T(1,128)S(1)} %bitcast.2, bf16[4,2,128,512]{3,2,1,0:T(8,128)(2,1)} %bitcast.3, ...), custom_call_target="tpu_custom_call" | custom-call | tf_op jit(solution)/shard_map/pallas_call | solution.py:637
  21.9 0.8 %pad_maximum_fusion = f32[256,512]{1,0:T(8,128)} fusion(f32[64,512]{1,0:T(8,128)S(1)} %get-tuple-element.12, f32[64,512]{1,0:T(8,128)S(1)} %get-tuple-element.11, f32[64,512]{1,0:T(8,128)S(1)} %get-tuple-element.10, f32[64,512]{1,0:T(8,128)S(1)} %get-tuple-element.9), kind=kLoop, calls=%fused_computation | loop fusion | flops 393216 | bytes 1048576 | tf_op jit(solution)/shard_map/concatenate | solution.py:685
Async XLA Ops:
  0.0 0.7 %copy-start = (f32[256]{0:T(256)S(1)}, f32[256]{0:T(256)}, u32[]{:S(2)}) copy-start(f32[256]{0:T(256)} %param.9) | copy-start | bytes 3076

commit v7 on v6

--- a/solution.py
+++ b/solution.py
@@ -133,7 +133,7 @@
     return two_parts(forward, 0), two_parts(inverse, 1)
 
 
-OUTS = 4
+OUTS = 2
 
 
 def block_kernel(
@@ -145,8 +145,6 @@
     tables_hbm,
     out_a,
     out_b,
-    out_c,
-    out_d,
     values_ref,
     gates_ref,
     taps_ref,
@@ -547,7 +545,7 @@
         def _():
             pl.semaphore_wait(ch_ready.at[other], 1)
 
-    outs = (out_a, out_b, out_c, out_d)
+    outs = (out_a, out_b)
     out_rows = out_a.shape[0]
     g_copies, direct, relayed = [], {}, {}
     for load in loads[3:5]:

time: 22.8 us -> 22.8 us (level)
  no operation moved by 1% of the time
where the time goes in v7:
time: 22.8 us; the launch traced here: 22.7 us
  Pallas kernels  21.2 us (93%)
  other arithmetic  0.83 us (4%)
  local copies, waits for them, and re-layouts  0.68 us (3%)
    pallas_call x1, Pallas kernels, block_body(): pl.pallas_call(block_kernel, out_shape=[jax.ShapeDtypeStruct((block_rows...  21.2 us
    concatenate x1, other arithmetic, block_body(): return jnp.concatenate(outs, axis=0)  0.83 us
    unnamed x2, local copies, waits for them, and re-layouts  0.68 us

profile of v7, /device:TPU:25, one launch (start us, length us, event | category | flops | bytes accessed | tf_op | source)
XLA Modules:
  0.0 22.7 jit_solution(17977863305623282059)
XLA Ops:
  0.0 0.0 copy-start
  0.0 0.7 %copy-done = f32[256]{0:T(256)S(1)} copy-done((f32[256]{0:T(256)S(1)}, f32[256]{0:T(256)}, u32[]{:S(2)}) %copy-start) | copy-done | bytes 1048
  0.7 21.2 %shard_map.64 = (f32[128,512]{1,0:T(8,128)S(1)}, f32[128,512]{1,0:T(8,128)S(1)}) custom-call(f32[256,256]{1,0:T(8,128)} %values_hbm.1, f32[256,256]{1,0:T(8,128)} %gates_hbm.1, f32[512,256]{1,0:T(8,128)} %taps_hbm.1, f32[1,256]{1,0:T(1,128)S(1)} %bitcast.2, bf16[4,2,128,512]{3,2,1,0:T(8,128)(2,1)} %bitcast.3, bf16[768,256]{1,0:T(8,128)(2,1)} %constant.2.clone.tables_hbm), custom_call_target="tpu_custom_call" | custom-call | tf_op jit(solution)/shard_map/pallas_call | solution.py:635
  21.9 0.8 %pad_maximum_fusion = f32[256,512]{1,0:T(8,128)} fusion(f32[128,512]{1,0:T(8,128)S(1)} %get-tuple-element.8, f32[128,512]{1,0:T(8,128)S(1)} %get-tuple-element.7), kind=kLoop, calls=%fused_computation | loop fusion | flops 131072 | bytes 1048576 | tf_op jit(solution)/shard_map/concatenate | solution.py:683
Async XLA Ops:
  0.0 0.7 %copy-start = (f32[256]{0:T(256)S(1)}, f32[256]{0:T(256)}, u32[]{:S(2)}) copy-start(f32[256]{0:T(256)} %param.9) | copy-start | bytes 3076
